TPU v7x, 128 devices: a whole 4x4x4 slice. The times are simulated.
128 devices in a mesh: band: 32 (over z, x, core), sub: 4 (over y).
Axes of the slice: x: 4, y: 4, z: 4, core: 2. Of those that a mesh axis runs over, the one named last changes fastest.
Arguments:
- grad_pred: bfloat16 [227, 98304], P(None, ('band', 'sub')), may hold values from -6 to 6
- grid_latent: bfloat16 [98304, 512], P(('band', 'sub')), may hold values from -6 to 6
- mesh_latent: bfloat16 [40960, 512], P(('band', 'sub')), may hold values from -6 to 6
- send_slot: int32 [98304], P(('band', 'sub')), may hold values from 0 to 2303, as said below
- edge_src: int32 [3, 294912], P(None, ('band', 'sub')), may hold values from 0 to 40959, as said below
- w_mesh: bfloat16 [512, 512], replicated, may hold values from -0.25 to 0.25
- w_grid: bfloat16 [512, 512], replicated, may hold values from -0.25 to 0.25
- w_msg: bfloat16 [512, 512], replicated, may hold values from -0.25 to 0.25
- w_out: bfloat16 [512, 227], replicated, may hold values from -0.25 to 0.25
Outputs:
- mesh_grad: bfloat16 [40960, 512], P(('band', 'sub'))
- grad_w_mesh: float32 [512, 512], replicated
- grad_w_grid: float32 [512, 512], replicated
- grad_w_msg: float32 [512, 512], replicated
- grad_w_out: float32 [512, 227], replicated
Inputs may be any that keep to these rules, and one draw needn't show every extreme that they name: For grid point p on latitude-major device i, send_slot[p] = j * 18 + r names patch-major device j and a rank r. On one device i the values are distinct, and for each j the ranks used are 0 to the count of i's points sent to j minus 1. Every such count is at most 18, and 18 is reached in every draw. Every grid point thereby gets one patch-major slot; live slots of each source stand at the front of its block of 18. One patch-major device holds at most 1920 live slots, reached on some device in every draw. `edge_src`: A slot on patch-major device j, of band b = j // 4, names senders in patch b only: mesh rows b * 1280 to (b + 1) * 1280 - 1. Entries of empty slots lie in that range too and are not read.
All inputs are finite; a program needn't handle non-finite values.
Results may differ from a plain program's by a relative error of at most 0.0076.
Values may be sent and summed in bfloat16 or wider, within the bound.
A program may use at most 128 MiB of HBM per device.

v0:
```python
import math

import jax
import jax.numpy as jnp
from jax import lax
from jax.sharding import PartitionSpec as P


def sent_to_all(x, axis):
    copies = jnp.broadcast_to(x, (lax.axis_size(axis), *x.shape))
    return lax.all_to_all(copies, axis, split_axis=0, concat_axis=0, tiled=True)


def laid_out(blocks, dim):
    shape = list(blocks.shape[1:])
    shape[dim] *= blocks.shape[0]
    return jnp.moveaxis(blocks, 0, dim).reshape(shape)


def collect(x, axis, dim):
    blocks = sent_to_all(x, axis)
    return laid_out(blocks, dim)


def cut_along(x, dim, devices):
    before, after = (x.shape[:dim], x.shape[dim + 1 :])
    return jnp.moveaxis(x.reshape(*before, devices, -1, *after), dim, 0)


def sent_and_summed(x, axis, dim):
    blocks = cut_along(x, dim, lax.axis_size(axis))
    arrived = lax.all_to_all(blocks, axis, split_axis=0, concat_axis=0, tiled=True)
    return arrived.sum(axis=0)


def latitude_weight(points, total):
    angle = jnp.pi * ((points.astype(jnp.float32) + 0.5) / total - 0.5)
    return 0.5 * jnp.pi * jnp.cos(angle)


def silu_slope(value):
    sigma = jax.nn.sigmoid(value)
    return sigma * (1.0 + value * (1.0 - sigma))


def contract_rows(left, right):
    return lax.dot_general(
        left, right, (((0,), (0,)), ((), ())), preferred_element_type=jnp.float32
    )


def times_transpose(left, right):
    return lax.dot_general(
        left, right, (((1,), (1,)), ((), ())), preferred_element_type=jnp.float32
    )


def shards(grad_pred, grid_latent, mesh_latent, send_slot, edge_src, w_mesh, w_grid, w_msg, w_out):
    grid_rows = grid_latent.shape[0]
    width = grid_latent.shape[1]
    channels = grad_pred.shape[0]
    devices = lax.axis_size(("band", "sub"))
    capacity = 3 * grid_rows // devices
    total_points = grid_rows * devices
    own_index = lax.axis_index(("band", "sub"))
    points = own_index * grid_rows + jnp.arange(grid_rows, dtype=jnp.int32)
    weighted = (
        latitude_weight(points, total_points)[None, :] * grad_pred.astype(jnp.float32)
    ).astype(jnp.bfloat16)
    target = send_slot // capacity
    slot_rank = send_slot % capacity
    joined = jnp.concatenate([grid_latent, weighted.T], axis=1)
    row_width = width + channels
    send_buffer = (
        jnp.zeros((devices, capacity, row_width), jnp.bfloat16).at[target, slot_rank].set(joined)
    )
    received = lax.all_to_all(send_buffer, ("band", "sub"), split_axis=0, concat_axis=0, tiled=True)
    slots = devices * capacity
    slot_rows = received.reshape(slots, row_width)
    latent_rows = slot_rows[:, :width]
    grad_rows = slot_rows[:, width:]
    grid_proj = jnp.dot(latent_rows, w_grid, preferred_element_type=jnp.float32).astype(
        jnp.bfloat16
    )
    mesh_proj = jnp.dot(mesh_latent, w_mesh, preferred_element_type=jnp.float32).astype(
        jnp.bfloat16
    )
    patch_proj = collect(mesh_proj, "sub", 0)
    patch_size = patch_proj.shape[0]
    band_index = lax.axis_index("band")
    local_node = edge_src - band_index * patch_size
    grid_float = grid_proj.astype(jnp.float32)
    pre_acts = [
        patch_proj[local_node[corner]].astype(jnp.float32) + grid_float for corner in range(3)
    ]
    act_sum = (
        jax.nn.silu(pre_acts[0]) + jax.nn.silu(pre_acts[1]) + jax.nn.silu(pre_acts[2])
    ).astype(jnp.bfloat16)
    aggregate = jnp.dot(act_sum, w_msg, preferred_element_type=jnp.float32).astype(jnp.bfloat16)
    out_part = contract_rows(aggregate, grad_rows)
    agg_rows = times_transpose(grad_rows, w_out).astype(jnp.bfloat16)
    msg_part = contract_rows(act_sum, agg_rows)
    out_total = lax.psum(out_part, ("band", "sub"))
    msg_total = lax.psum(msg_part, ("band", "sub"))
    act_grad = times_transpose(agg_rows, w_msg)
    pre_grads = [(act_grad * silu_slope(pre)).astype(jnp.bfloat16) for pre in pre_acts]
    grid_proj_grad = (
        pre_grads[0].astype(jnp.float32)
        + pre_grads[1].astype(jnp.float32)
        + pre_grads[2].astype(jnp.float32)
    ).astype(jnp.bfloat16)
    node_part = jnp.zeros((patch_size, width), jnp.float32)
    for corner in range(3):
        node_part = node_part.at[local_node[corner]].add(pre_grads[corner].astype(jnp.float32))
    node_total = sent_and_summed(node_part, "sub", 0)
    grid_part = contract_rows(latent_rows, grid_proj_grad)
    mesh_proj_grad = node_total.astype(jnp.bfloat16)
    mesh_grad = times_transpose(mesh_proj_grad, w_mesh).astype(jnp.bfloat16)
    mesh_part = contract_rows(mesh_latent, mesh_proj_grad)
    grad_scale = 1.0 / math.sqrt(3.0 * total_points)
    grid_total = lax.psum(grid_part, ("band", "sub"))
    mesh_total = lax.psum(mesh_part, ("band", "sub"))
    return (
        mesh_grad,
        mesh_total * grad_scale,
        grid_total * grad_scale,
        msg_total * grad_scale,
        out_total * grad_scale,
    )


def solution(mesh):
    placed = (
        P(None, ("band", "sub")),
        P(("band", "sub"), None),
        P(("band", "sub"), None),
        P(("band", "sub")),
        P(None, ("band", "sub")),
        P(),
        P(),
        P(),
        P(),
    )
    return jax.shard_map(
        shards,
        mesh=mesh,
        in_specs=placed,
        out_specs=(P(("band", "sub"), None), P(), P(), P(), P()),
        check_vma=False,
    )
```

profile of v0, /device:TPU:1, one launch (start us, length us, event | category | flops | bytes accessed | tf_op | source)
XLA Modules:
  0.0 477.6 jit_solution(13658572427953720759)
XLA Ops:
  7.2 0.0 copy-start
  7.2 0.0 copy-start.10
  7.2 1.5 convolution_convert_fusion.4
  8.7 0.0 copy-start.13
  8.8 1.3 broadcast_in_dim.26
  10.0 5.0 %all-to-all-start.1 = ((bf16[4,320,512]{2,1,0:T(8,128)(2,1)}), bf16[4,320,512]{2,1,0:T(8,128)(2,1)S(1)}, u32[]{:S(2)}, u32[]{:S(2)}) async-start(bf16[4,320,512]{2,1,0:T(8,128)(2,1)} %broadcast_in_dim.26), calls=%async_computation.1 | async-start | bytes 2621440 | tf_op jit(solution)/shard_map/all_to_all | solution.py:11
  15.1 0.0 copy-done.10
  15.1 0.1 fusion.15
  15.1 0.2 copy.41
  15.3 0.0 copy-done.13
  15.4 1.2 pad_maximum_fusion
  16.6 2.1 broadcast_in_dim.11
  18.8 103.0 %scatter_fusion = bf16[128,18,739]{2,0,1:T(8,128)(2,1)} fusion(bf16[128,18,739]{2,0,1:T(8,128)(2,1)} %broadcast_in_dim.11, s32[768]{0:T(1024)S(1)} %fusion.23, bf16[768,739]{1,0:T(8,128)(2,1)S(1)} %pad_maximum_fusion), kind=kCustom, calls=%fused_computation.3 | custom fusion | bytes 3411456 | tf_op jit(solution)/shard_map/scatter | solution.py:75
  121.8 6.2 %copy.42 = bf16[128,18,739]{2,1,0:T(8,128)(2,1)} copy(bf16[128,18,739]{2,0,1:T(8,128)(2,1)} %scatter_fusion) | data formatting | bytes 6810624 | tf_op jit(solution)/shard_map/scatter | solution.py:75
  127.9 0.0 all-to-all-done.1
  127.9 11.8 %all-to-all-start = ((bf16[128,18,739]{2,1,0:T(8,128)(2,1)}), bf16[128,18,739]{2,1,0:T(8,128)(2,1)}, u32[]{:S(2)}, u32[]{:S(2)}) async-start(bf16[128,18,739]{2,1,0:T(8,128)(2,1)} %copy.42), calls=%async_computation | async-start | bytes 9437184 | tf_op jit(solution)/shard_map/all_to_all | solution.py:77
  139.7 0.0 copy-done.12
  139.7 0.1 fusion.20
  139.9 7.5 %gather_fusion.2 = bf16[2304,512]{1,0:T(8,128)(2,1)} fusion(bf16[1280,512]{1,0:T(8,128)(2,1)S(1)} %bitcast.33, s32[3072]{0:T(1024)S(1)} %get-tuple-element.43), kind=kCustom, calls=%fused_computation.2 | custom fusion | bytes 4727808 | tf_op jit(solution)/shard_map/gather | solution.py:94
  147.4 7.5 %gather_fusion.1 = bf16[2304,512]{1,0:T(8,128)(2,1)} fusion(bf16[1280,512]{1,0:T(8,128)(2,1)S(1)} %bitcast.34, s32[3072]{0:T(1024)S(1)} %get-tuple-element.44), kind=kCustom, calls=%fused_computation.1 | custom fusion | bytes 4727808 | tf_op jit(solution)/shard_map/gather | solution.py:94
  154.9 7.5 %gather_fusion = bf16[2304,512]{1,0:T(8,128)(2,1)} fusion(bf16[1280,512]{1,0:T(8,128)(2,1)S(1)} %bitcast.35, s32[3072]{0:T(1024)S(1)} %pad_clamp_fusion.2), kind=kCustom, calls=%fused_computation | custom fusion | bytes 4727808 | tf_op jit(solution)/shard_map/gather | solution.py:94
  162.4 0.0 copy-start.11
  162.4 35.8 %all-to-all-done = bf16[128,18,739]{2,1,0:T(8,128)(2,1)} async-done(((bf16[128,18,739]{2,1,0:T(8,128)(2,1)}), bf16[128,18,739]{2,1,0:T(8,128)(2,1)}, u32[]{:S(2)}, u32[]{:S(2)}) %all-to-all-start) | async-done | bytes 3405344 | tf_op jit(solution)/shard_map/all_to_all | solution.py:77
  198.2 0.0 copy-start.14
  198.2 7.0 %reshape.114 = bf16[2304,739]{1,0:T(8,128)(2,1)} reshape(bf16[128,18,739]{2,1,0:T(8,128)(2,1)} %all-to-all-done) | data formatting | bytes 6810624 | tf_op jit(solution)/shard_map/reshape | solution.py:79
  205.2 0.0 copy-done.11
  205.2 0.0 copy-start.2
  205.2 2.2 convolution_convert_fusion.2
  207.4 0.0 copy-done.14
  207.4 0.2 copy-done.2
  207.6 1.4 convolution_convert_fusion.1
  209.1 0.0 copy-done.3
  209.1 0.0 copy-done
  209.1 1.1 copy-done.4
  210.1 0.7 copy-done.5
  210.8 0.7 copy-done.6
  211.6 9.0 %multiply_convert_fusion = (bf16[2304,512]{1,0:T(8,128)(2,1)}, bf16[2304,512]{1,0:T(8,128)(2,1)}, bf16[2304,512]{1,0:T(8,128)(2,1)}, bf16[2304,512]{1,0:T(8,128)(2,1)}) fusion(bf16[2304,512]{1,0:T(8,128)(2,1)S(1)} %convolution_convert_fusion.1, bf16[2304,512]{1,0:T(8,128)(2,1)S(1)} %copy-done.4, bf16[2304,512]{1,0:T(8,128)(2,1)S(1)} %copy-done.5, ...), kind=kOutput, calls=%fused_computation.20 | convolution fusion | flops 1255145472 | bytes 21757952 | tf_op jit(solution)/shard_map/dot_general | solution.py:53
  220.6 17.0 %scatter_custom_fusion.1 = f32[1280,512]{1,0:T(8,128)S(1)} fusion(s32[2304]{0:T(1024)S(1)} %get-tuple-element.32, bf16[2304,512]{1,0:T(8,128)(2,1)} %get-tuple-element.40, f32[]{:T(128)} %constant.20.clone.1), kind=kCustom, calls=%fused_computation.16 | custom fusion | flops 2359296 | bytes 4980740 | tf_op jit(solution)/shard_map/scatter-add | solution.py:114
  237.6 17.6 %scatter_custom_fusion.2 = f32[1280,512]{1,0:T(8,128)S(1)} fusion(f32[1280,512]{1,0:T(8,128)S(1)} %scatter_custom_fusion.1, s32[2304]{0:T(1024)S(1)} %get-tuple-element.31, bf16[2304,512]{1,0:T(8,128)(2,1)} %get-tuple-element.38), kind=kCustom, calls=%fused_computation.14 | custom fusion | flops 2359296 | bytes 4980736 | tf_op jit(solution)/shard_map/scatter-add | solution.py:114
  255.2 17.4 %scatter_custom_fusion.3 = f32[1280,512]{1,0:T(8,128)S(1)} fusion(f32[1280,512]{1,0:T(8,128)S(1)} %scatter_custom_fusion.2, s32[2304]{0:T(1024)S(1)} %get-tuple-element.30, bf16[2304,512]{1,0:T(8,128)(2,1)} %get-tuple-element.37), kind=kCustom, calls=%fused_computation.11 | custom fusion | flops 2359296 | bytes 4980736 | tf_op jit(solution)/shard_map/scatter-add | solution.py:114
  272.6 0.0 copy-start.1
  272.6 1.5 copy-done.1
  274.1 3.7 all-to-all-start.2
  277.7 0.3 all-reduce.3.cloned.1.call-start
  278.0 4.8 %fusion.24 = f32[512,512]{0,1:T(8,128)} fusion(bf16[2304,512]{1,0:T(8,128)(2,1)} %get-tuple-element.39, bf16[2304,512]{1,0:T(8,128)(2,1)} %copy-done.3), kind=kOutput, calls=%fused_computation.74 | convolution fusion | flops 1207959552 | bytes 5767168 | tf_op jit(solution)/shard_map/dot_general | solution.py:47
  282.8 4.7 fusion.12
  287.5 6.2 %fusion.7 = f32[512,512]{0,1:T(8,128)} fusion(bf16[2304,512]{1,0:T(8,128)(2,1)} %get-tuple-element.37, bf16[2304,512]{1,0:T(8,128)(2,1)} %get-tuple-element.38, bf16[2304,512]{1,0:T(8,128)(2,1)} %get-tuple-element.40, bf16[2304,739]{1,0:T(8,128)(2,1)} %reshape.114), kind=kOutput, calls=%fused_computation.29 | convolution fusion | flops 1215037440 | bytes 10485760 | tf_op jit(solution)/shard_map/dot_general | solution.py:47
  293.7 16.3 %all-to-all-done.2 = f32[4,320,512]{2,1,0:T(8,128)S(1)} async-done(((f32[4,320,512]{2,1,0:T(8,128)}), f32[4,320,512]{2,1,0:T(8,128)S(1)}, u32[]{:S(2)}, u32[]{:S(2)}) %all-to-all-start.2) | async-done | bytes 2621472 | tf_op jit(solution)/shard_map/all_to_all | solution.py:32
  310.0 0.3 reduce_sum.9
  310.4 0.0 copy-start.7
  310.4 2.5 convolution_bitcast_fusion
  312.8 0.0 all-reduce.3.cloned.1.call-update
  312.9 0.0 copy-done.7
  312.9 1.1 convolution_convert_fusion.3
  314.0 149.2 %all-reduce.3.cloned.1.call-done = (f32[512,512]{0,1:T(8,128)}, f32[512,512]{0,1:T(8,128)}, f32[512,512]{0,1:T(8,128)}, f32[512,227]{0,1:T(8,128)}) async-done(((f32[512,512]{0,1:T(8,128)}, f32[512,512]{0,1:T(8,128)}, f32[512,512]{0,1:T(8,128)}, f32[512,227]{0,1:T(8,128)}), (f32[512,512]{0,1:T(8,128)}, f32[512,512]{0,1:T(8,128)}, f32[512,512]{0,1:T(8,128)}, ...) | async-done | bytes 3610640 | tf_op jit(solution)/shard_map/psum | solution.py:122
  463.2 1.4 broadcast_multiply_fusion.2
  464.6 1.3 copy.45
  465.9 0.0 copy-done.9
  465.9 0.8 broadcast_multiply_fusion.3
  466.7 1.3 broadcast_multiply_fusion.1
  468.1 1.3 copy.46
  469.4 0.0 copy-done.8
  469.4 0.1 broadcast_multiply_fusion
  469.5 1.3 copy.47
  (13 shorter events, 0.1 us)
Async XLA Ops:
  7.2 201.9 %copy-start = (bf16[512,512]{1,0:T(8,128)(2,1)S(1)}, bf16[512,512]{1,0:T(8,128)(2,1)}, u32[]{:S(2)}) copy-start(bf16[512,512]{1,0:T(8,128)(2,1)} %param.16) | copy-start | bytes 1572868
  7.2 7.9 %copy-start.10 = (bf16[227,768]{1,0:T(8,128)(2,1)S(1)}, bf16[227,768]{1,0:T(8,128)(2,1)}, u32[]{:S(2)}) copy-start(bf16[227,768]{1,0:T(8,128)(2,1)} %param.9) | copy-start | bytes 1046020
  8.7 6.6 %copy-start.13 = (s32[768]{0:T(1024)S(1)}, s32[768]{0:T(1024)}, u32[]{:S(2)}) copy-start(s32[768]{0:T(1024)} %param.12) | copy-start | bytes 9220
  10.0 117.9 %all-to-all-start.1 = ((bf16[4,320,512]{2,1,0:T(8,128)(2,1)}), bf16[4,320,512]{2,1,0:T(8,128)(2,1)S(1)}, u32[]{:S(2)}, u32[]{:S(2)}) async-start(bf16[4,320,512]{2,1,0:T(8,128)(2,1)} %broadcast_in_dim.26), calls=%async_computation.1 | async-start | bytes 2621440 | tf_op jit(solution)/shard_map/all_to_all | solution.py:11
  127.9 11.8 %copy-start.12 = (s32[3,2304]{1,0:T(4,128)S(1)}, s32[3,2304]{1,0:T(4,128)}, u32[]{:S(2)}) copy-start(s32[3,2304]{1,0:T(4,128)} %param.13) | copy-start | bytes 82948
  127.9 70.3 %all-to-all-start = ((bf16[128,18,739]{2,1,0:T(8,128)(2,1)}), bf16[128,18,739]{2,1,0:T(8,128)(2,1)}, u32[]{:S(2)}, u32[]{:S(2)}) async-start(bf16[128,18,739]{2,1,0:T(8,128)(2,1)} %copy.42), calls=%async_computation | async-start | bytes 9437184 | tf_op jit(solution)/shard_map/all_to_all | solution.py:77
  162.4 42.8 %copy-start.11 = (bf16[512,227]{0,1:T(8,128)(2,1)S(1)}, bf16[512,227]{0,1:T(8,128)(2,1)}, u32[]{:S(2)}) copy-start(bf16[512,227]{0,1:T(8,128)(2,1)} %param.17) | copy-start | bytes 697348
  198.2 9.2 %copy-start.14 = (bf16[512,512]{1,0:T(8,128)(2,1)S(1)}, bf16[512,512]{1,0:T(8,128)(2,1)}, u32[]{:S(2)}) copy-start(bf16[512,512]{1,0:T(8,128)(2,1)} %param.15) | copy-start | bytes 1572868
  205.2 2.4 copy-start.2
  207.6 1.4 copy-start.3
  207.6 2.5 copy-start.4
  207.6 3.2 copy-start.5
  207.6 3.9 copy-start.6
  272.6 1.5 copy-start.1
  274.1 36.0 %all-to-all-start.2 = ((f32[4,320,512]{2,1,0:T(8,128)}), f32[4,320,512]{2,1,0:T(8,128)S(1)}, u32[]{:S(2)}, u32[]{:S(2)}) async-start(f32[4,320,512]{2,1,0:T(8,128)} %bitcast.36), calls=%async_computation.2 | async-start | bytes 5242880 | tf_op jit(solution)/shard_map/all_to_all | solution.py:32
  277.7 185.5 %all-reduce.3.cloned.1.call-start = ((), (), s32[]{:S(2)}) async-start(), calls=%async_computation.3 | async-start | bytes 7241728 | tf_op jit(solution)/shard_map/psum | solution.py:122
  310.4 2.5 copy-start.7
  463.2 2.7 copy-start.9
  465.9 3.5 copy-start.8
Sparse Core Ops, SparseCore 0:
  313.0 150.1 all-reduce.2
where the time goes:
time: 482 us; the launch traced here: 478 us
  waiting for transfers between devices  201 us (42%)
  local copies, waits for them, and re-layouts  150 us (31%)
  other arithmetic  57.4 us (12%)
  matrix products  33.4 us (7%)
  starting transfers between devices  20.7 us (4%)
  between operations  14.3 us (3%)
    psum x1, waiting for transfers between devices, shards(): mesh_total = lax.psum(mesh_part, ('band', 'sub'))  149 us
    scatter x2, local copies, waits for them, and re-layouts, shards(): jnp.zeros((devices, capacity, row_width), jnp.bfloat16)  109 us
    scatter-add x3, other arithmetic, shards(): node_part.at[local_node[corner]].add(pre_grads[corner].astype(jnp.float32))  52 us
    all_to_all x1, waiting for transfers between devices, shards(): lax.all_to_all(send_buffer, ('band', 'sub'), split_axis=0, concat_axis=0,...  35.8 us
    gather x3, local copies, waits for them, and re-layouts, shards(): patch_proj[local_node[corner]].astype(jnp.float32) + grid_float  22.5 us
    dot_general x4, matrix products, contract_rows(): lax.dot_general(left, right, (((0,), (0,)), ((), ())), preferred_element_...  18.1 us
    all_to_all x1, waiting for transfers between devices, sent_and_summed(): lax.all_to_all(blocks, axis, split_axis=0, concat_axis=0, tiled=True)  16.3 us
    dot_general x3, matrix products, times_transpose(): lax.dot_general(left, right, (((1,), (1,)), ((), ())), preferred_element_...  12.3 us
  transfers between devices with their start and end apart: 4, of which 3 were waited for; matrix products, arithmetic and copies ran while one was open for 32% of the time, Pallas kernels for 0%

commit v1 on v0

v1 whole, which is shorter than its diff:
```python
import functools
import math

import jax
import jax.numpy as jnp
from jax import lax
from jax.experimental import pallas as pl
from jax.experimental.pallas import tpu as pltpu
from jax.sharding import PartitionSpec as P

MESH = pl.DeviceIdType.MESH
BF, F32 = jnp.bfloat16, jnp.float32
MAIN, OVER = 16, 2
CAP = MAIN + OVER
NDEV = 128
NN = (((1,), (0,)), ((), ()))
NT = (((1,), (1,)), ((), ()))
TN = (((0,), (0,)), ((), ()))
STRIDE, INVERSE = 37, 45


def dot(a, b, dims):
    return lax.dot_general(a, b, dims, preferred_element_type=F32)


def place():
    band, sub = lax.axis_index("band"), lax.axis_index("sub")
    return band // 8, (band // 2) % 4, band % 2, sub


def offset(d):
    e = (d * STRIDE) % NDEV
    return (e // 16) % 4, (e // 4) % 4, e // 64, e % 4


def peer(d):
    z, x, c, y = place()
    dz, dx, dc, dy = offset(d)
    return ((z + dz) % 4) * 8 + ((x + dx) % 4) * 2 + (c + dc) % 2, (y + dy) % 4


def source(d):
    z, x, c, y = place()
    dz, dx, dc, dy = offset(d)
    band = ((z - dz + 4) % 4) * 8 + ((x - dx + 4) % 4) * 2 + (c + dc) % 2
    return band * 4 + (y - dy + 4) % 4


ROWS = 256
GROUPS = NDEV * CAP // ROWS
BLOCKS = ROWS // MAIN
CHIPS = 64


def chip_peer(q):
    z, x, c, y = place()
    p = (q * 37) % CHIPS
    z, x, y = (z + p // 16) % 4, (x + (p // 4) % 4) % 4, (y + p % 4) % 4
    return (z * 8 + x * 2 + c, y), (z * 4 + x) * 4 + y


def remote(src, dst, send, recv, device):
    return pltpu.make_async_remote_copy(
        src_ref=src,
        dst_ref=dst,
        send_sem=send,
        recv_sem=recv,
        device_id=device,
        device_id_type=MESH,
    )


def kernel(
    grad_ref,
    latent_ref,
    mesh_ref,
    slot_ref,
    index_ref,
    w_mesh_ref,
    w_grid_ref,
    w_msg_ref,
    w_out_ref,
    sums_ref,
    proj_ref,
    weighted,
    main_send,
    over_send,
    main_recv,
    over_recv,
    patch,
    table,
    back,
    node,
    node_send,
    node_recv,
    rows_ref,
    pre_grad,
    part,
    pair_recv,
    rs_send,
    rs_recv,
    ag_send,
    main_ssem,
    main_rsem,
    ssem,
    rsem,
):
    z, x, c, y = place()
    band = lax.axis_index("band")
    sibling = (band + 1 - 2 * c, y)
    bar = pltpu.get_barrier_semaphore()

    def greet(d, carry):
        pl.semaphore_signal(bar, inc=1, device_id=peer(d), device_id_type=MESH)
        return carry

    lax.fori_loop(1, NDEV, greet, 0)

    channels, points = grad_ref.shape
    me = band * 4 + y
    lane = lax.broadcasted_iota(jnp.int32, (1, points), 1)
    total = points * NDEV
    angle = jnp.pi * (((me * points + lane).astype(F32) + 0.5) / total - 0.5)
    weight = 0.5 * jnp.pi * jnp.cos(angle)
    weighted[...] = jnp.zeros_like(weighted)
    weighted[0:channels, :] = (weight * grad_ref[...].astype(F32)).astype(BF)
    slot = slot_ref[...]
    j = (slot * 3641) >> 16
    r = slot - j * CAP
    e = (
        ((j - y) & 3)
        + 4 * (((j >> 3) - x) & 3)
        + 16 * (((j >> 5) - z) & 3)
        + 64 * (((j >> 2) - c) & 1)
    )
    d = (e * INVERSE) & (NDEV - 1)
    at_main = jnp.where(r < MAIN, d * MAIN + r, -1)
    at_over = jnp.where(r >= MAIN, d * OVER + r - MAIN, -1)
    row = lax.broadcasted_iota(jnp.int32, (ROWS, points), 0)

    def pick(at, base):
        hot = jnp.where(row == at - base, 1.0, 0.0).astype(BF)
        lat = dot(hot, latent_ref[...], NN).astype(BF)
        gr = dot(hot, weighted[...], NT).astype(BF)
        return lat, gr

    lat, gr = pick(at_over, 0)
    over_send[:, :, 0:512] = lat.reshape(NDEV, OVER, 512)
    over_send[:, :, 512:768] = gr.reshape(NDEV, OVER, 256)
    over_recv[0] = over_send[0]
    patch[y] = mesh_ref[...]

    def pick_main(g):
        lat, gr = pick(at_main, g * ROWS)
        blocks = pl.ds(g * BLOCKS, BLOCKS)
        main_send[blocks, :, 0:512] = lat.reshape(BLOCKS, MAIN, 512)
        main_send[blocks, :, 512:768] = gr.reshape(BLOCKS, MAIN, 256)

    pick_main(0)
    main_recv[0] = main_send[0]
    pl.semaphore_wait(bar, NDEV - 1)

    def patch_copy(k):
        return remote(
            mesh_ref, patch.at[y], ssem.at[0], rsem.at[0], (band, (y + k) % 4)
        )

    for k in (1, 2, 3):
        patch_copy(k).start()

    def send_over(d, carry):
        remote(
            over_send.at[d], over_recv.at[d], ssem.at[1], rsem.at[1], peer(d)
        ).start()
        return carry

    lax.fori_loop(1, NDEV, send_over, 0)

    def send_main(d, carry):
        remote(
            main_send.at[d], main_recv.at[d], main_ssem.at[0], main_rsem.at[d // BLOCKS], peer(d)
        ).start()
        return carry

    lax.fori_loop(1, BLOCKS, send_main, 0)

    def prep_group(g, carry):
        pick_main(g)
        lax.fori_loop(g * BLOCKS, (g + 1) * BLOCKS, send_main, 0)
        return carry

    lax.fori_loop(1, GROUPS - 1, prep_group, 0)

    back[...] = jnp.zeros_like(back)
    back[:, 0:channels] = dot(w_msg_ref[...], w_out_ref[...], NN).astype(BF)
    node[...] = jnp.zeros_like(node)
    part[...] = jnp.zeros_like(part)
    remote(
        patch.at[pl.ds(0, 3)], patch.at[pl.ds(0, 3)], ssem.at[0], rsem.at[0], sibling
    ).wait_recv()
    for k in range(4):
        table[pl.ds(k * 320, 320), :] = dot(patch[k], w_mesh_ref[...], NN).astype(BF)
    size = table.shape[0]

    def group(g):
        latent, grad = rows_ref[:, 0:512], rows_ref[:, 512:768]
        grid_proj = dot(latent, w_grid_ref[...], NN).astype(BF).astype(F32)
        act_grad = dot(grad, back[...], NT)
        index = index_ref[g]
        column = index.T
        node_col = lax.broadcasted_iota(jnp.int32, (ROWS, size), 1)
        node_row = lax.broadcasted_iota(jnp.int32, (size, ROWS), 0)
        act = jnp.zeros((ROWS, 512), F32)
        total = jnp.zeros((ROWS, 512), F32)
        for k in range(3):
            hot = jnp.where(node_col == column[:, k : k + 1], 1.0, 0.0).astype(BF)
            pre = dot(hot, table[...], NN) + grid_proj
            sigma = 0.5 * jnp.tanh(0.5 * pre) + 0.5
            value = pre * sigma
            act += value
            grad_k = (act_grad * (sigma + value * (1.0 - sigma))).astype(BF)
            total += grad_k.astype(F32)
            pre_grad[pl.ds(k * ROWS, ROWS), :] = grad_k
        act = act.astype(BF)
        moment = dot(act, grad, TN)
        part[0, :, 512:640] += moment[:, 0:128]
        part[1, :, 512:640] += moment[:, 128:256]
        part[1, :, 0:512] += dot(latent, total.astype(BF), TN)
        hots = [
            jnp.where(node_row == index[k : k + 1, :], 1.0, 0.0).astype(BF)
            for k in range(3)
        ]
        node[...] += dot(jnp.concatenate(hots, axis=1), pre_grad[...], NN)

    def await_main(g, first, count):
        blocks = pl.ds(first, count)
        remote(
            main_send.at[blocks], main_recv.at[blocks], main_ssem.at[0], main_rsem.at[g], sibling
        ).wait_recv()

    def step(g, carry):
        @pl.when(g == 0)
        def _():
            blocks = pl.ds(1, NDEV - 1)
            remote(
                over_send.at[blocks], over_recv.at[blocks], ssem.at[1], rsem.at[1], sibling
            ).wait_recv()
            rows_ref[...] = over_recv[...].reshape(ROWS, 768)

        @pl.when(g == 1)
        def _():
            await_main(0, 1, BLOCKS - 1)

        @pl.when(g > 1)
        def _():
            await_main(g - 1, (g - 1) * BLOCKS, BLOCKS)

        @pl.when(g > 0)
        def _():
            blocks = pl.ds((g - 1) * BLOCKS, BLOCKS)
            rows_ref[...] = main_recv[blocks, :, :].reshape(ROWS, 768)

        group(g)
        return carry

    lax.fori_loop(0, GROUPS, step, 0)

    def node_copy(k):
        to = (y + k) % 4
        return remote(
            node_send.at[to], node_recv.at[k - 1], ssem.at[2], rsem.at[2], (band, to)
        )

    for k in range(4):
        node_send[k] = node[pl.ds(k * 320, 320), :].astype(BF)
    mesh_part = dot(patch[0], node_send[0], TN)
    for k in (1, 2, 3):
        mesh_part += dot(patch[k], node_send[k], TN)
    part[0, :, 0:512] = mesh_part
    pair = remote(part.at[1 - c], pair_recv, ssem.at[3], rsem.at[3], sibling)
    pair.start()
    for k in (1, 2, 3):
        node_copy(k).start()
    pair.wait_recv()
    rs_send[...] = (part[c] + pair_recv[...]).astype(BF).reshape(CHIPS, 8, 640)

    def scatter(q, carry):
        device, chip = chip_peer(q)
        remote(rs_send.at[chip], rs_recv.at[q], ssem.at[4], rsem.at[4], device).start()
        return carry

    lax.fori_loop(1, CHIPS, scatter, 0)
    own, chip = chip_peer(0)
    rs_recv[0] = rs_send[chip]

    remote(
        node_send.at[pl.ds(0, 3)], node_recv, ssem.at[2], rsem.at[2], sibling
    ).wait_recv()
    mine = node[pl.ds(y * 320, 320), :]
    proj_ref[...] = (
        mine + node_recv[0].astype(F32) + node_recv[1].astype(F32) + node_recv[2].astype(F32)
    ).astype(BF)

    others = pl.ds(1, CHIPS - 1)
    remote(
        rs_send.at[others], rs_recv.at[others], ssem.at[4], rsem.at[4], sibling
    ).wait_recv()
    scale = 1.0 / math.sqrt(3.0 * points * NDEV)
    ag_send[...] = (jnp.sum(rs_recv[...].astype(F32), axis=0) * scale).astype(BF)
    sums_ref[c, chip] = ag_send[...]

    def gather(q, carry):
        device, _ = chip_peer(q)
        remote(ag_send, sums_ref.at[c, chip], ssem.at[5], rsem.at[5], device).start()
        return carry

    lax.fori_loop(1, CHIPS, gather, 0)
    most = sums_ref.at[c, pl.ds(0, CHIPS - 1)]
    remote(most, most, ssem.at[5], rsem.at[5], sibling).wait_recv()
    share = remote(sums_ref.at[c], sums_ref.at[c], ssem.at[6], rsem.at[6], sibling)
    share.start()

    three = node_send.at[pl.ds(0, 3)]
    remote(patch.at[pl.ds(0, 3)], patch.at[pl.ds(0, 3)], ssem.at[0], rsem.at[0], sibling).wait_send()
    blocks = pl.ds(1, NDEV - 1)
    remote(over_send.at[blocks], over_recv.at[blocks], ssem.at[1], rsem.at[1], sibling).wait_send()
    remote(main_send.at[blocks], main_recv.at[blocks], main_ssem.at[0], main_rsem.at[0], sibling).wait_send()
    remote(three, node_recv, ssem.at[2], rsem.at[2], sibling).wait_send()
    pair.wait_send()
    remote(rs_send.at[others], rs_recv.at[others], ssem.at[4], rsem.at[4], sibling).wait_send()
    remote(most, most, ssem.at[5], rsem.at[5], sibling).wait_send()
    share.wait()


def final_kernel(sums_ref, proj_ref, w_mesh_ref, w_msg_ref, w_out_ref, node_ref, mesh_ref, grid_ref, msg_ref, out_ref):
    node_ref[...] = dot(proj_ref[...], w_mesh_ref[...], NT).astype(BF)
    mesh_ref[...] = sums_ref[0, :, :, 0:512].astype(F32).reshape(512, 512)
    grid_ref[...] = sums_ref[1, :, :, 0:512].astype(F32).reshape(512, 512)
    low = sums_ref[0, :, :, 512:640].astype(F32).reshape(512, 128)
    high = sums_ref[1, :, :, 512:640].astype(F32).reshape(512, 128)
    moment = jnp.concatenate([low, high], axis=1)[:, 0:227].astype(BF)
    msg_ref[...] = dot(moment, w_out_ref[...], NT)
    out_ref[...] = dot(w_msg_ref[...], moment, TN)


def shards(grad_pred, grid_latent, mesh_latent, send_slot, edge_src, w_mesh, w_grid, w_msg, w_out):
    band = lax.axis_index("band")
    order = source(jnp.arange(NDEV, dtype=jnp.int32))
    local = (edge_src - band * 1280).reshape(3, NDEV, CAP)[:, order, :]
    head = local[:, :, :MAIN].reshape(3, GROUPS - 1, ROWS).transpose(1, 0, 2)
    tail = local[:, :, MAIN:].reshape(3, 1, ROWS).transpose(1, 0, 2)
    index = jnp.concatenate([tail, head], axis=0)
    index = jnp.pad(index, ((0, 0), (0, 5), (0, 0)))
    vmem = pltpu.VMEM
    sums, proj = pl.pallas_call(
        kernel,
        out_shape=[
            jax.ShapeDtypeStruct((2, CHIPS, 8, 640), BF),
            jax.ShapeDtypeStruct((320, 512), BF),
        ],
        scratch_shapes=[
            vmem((256, 768), BF),
            vmem((NDEV, MAIN, 768), BF),
            vmem((NDEV, OVER, 768), BF),
            vmem((NDEV, MAIN, 768), BF),
            vmem((NDEV, OVER, 768), BF),
            vmem((4, 320, 512), BF),
            vmem((1280, 512), BF),
            vmem((512, 256), BF),
            vmem((1280, 512), F32),
            vmem((4, 320, 512), BF),
            vmem((3, 320, 512), BF),
            vmem((ROWS, 768), BF),
            vmem((3 * ROWS, 512), BF),
            vmem((2, 512, 640), F32),
            vmem((512, 640), F32),
            vmem((CHIPS, 8, 640), BF),
            vmem((CHIPS, 8, 640), BF),
            vmem((8, 640), BF),
            pltpu.SemaphoreType.DMA((1,)),
            pltpu.SemaphoreType.DMA((GROUPS - 1,)),
            pltpu.SemaphoreType.DMA((7,)),
            pltpu.SemaphoreType.DMA((7,)),
        ],
        compiler_params=pltpu.CompilerParams(
            collective_id=0, has_side_effects=True, vmem_limit_bytes=63 * 2**20
        ),
    )(
        grad_pred,
        grid_latent,
        mesh_latent,
        send_slot.reshape(1, -1),
        index,
        w_mesh,
        w_grid,
        w_msg,
        w_out,
    )
    return pl.pallas_call(
        final_kernel,
        out_shape=[
            jax.ShapeDtypeStruct((320, 512), BF),
            jax.ShapeDtypeStruct((512, 512), F32),
            jax.ShapeDtypeStruct((512, 512), F32),
            jax.ShapeDtypeStruct((512, 512), F32),
            jax.ShapeDtypeStruct((512, 227), F32),
        ],
        compiler_params=pltpu.CompilerParams(vmem_limit_bytes=40 * 2**20),
    )(sums, proj, w_mesh, w_msg, w_out)


def solution(mesh):
    both = ("band", "sub")
    placed = (P(None, both), P(both, None), P(both, None), P(both), P(None, both))
    return jax.shard_map(
        shards,
        mesh=mesh,
        in_specs=placed + (P(),) * 4,
        out_specs=(P(both, None), P(), P(), P(), P()),
        check_vma=False,
    )
```

time: 482 us -> 148 us (0.31)
  waiting for transfers between devices: 201 us -> 0 us
  local copies, waits for them, and re-layouts: 150 us -> 8.69 us
  Pallas kernels: 0 us -> 137 us
  other arithmetic: 57.4 us -> 0.83 us
  matrix products: 33.4 us -> 0 us
  starting transfers between devices: 20.7 us -> 0 us
  between operations: 14.3 us -> 0.77 us
    psum x1 -> x0, waiting for transfers between devices: 149 us -> none  [shards(): mesh_total = lax.psum(mesh_part, ('band', 'sub'))]
    pallas_call x0 -> x2, Pallas kernels: none -> 137 us  [the longest x1 135 us: shards(): pl.pallas_call(kernel, out_shape=[jax.ShapeDtypeStruct((2, CHIPS, 8, 640)...]
    scatter x2 -> x0, local copies, waits for them, and re-layouts: 109 us -> none  [shards(): jnp.zeros((devices, capacity, row_width), jnp.bfloat16)]
    all_to_all x3 -> x0, waiting for transfers between devices: 52.1 us -> none  [the longest x1 35.8 us: shards(): lax.all_to_all(send_buffer, ('band', 'sub'), split_axis=0, concat_axis=0,...]
    scatter-add x3 -> x0, other arithmetic: 52 us -> none  [shards(): node_part.at[local_node[corner]].add(pre_grads[corner].astype(jnp.float32))]
    dot_general x9 -> x0, matrix products: 33.4 us -> none  [the longest x4 18.1 us: contract_rows(): lax.dot_general(left, right, (((0,), (0,)), ((), ())), preferred_element_...]
    gather x3 -> x1, local copies, waits for them, and re-layouts: 22.5 us -> 0.75 us  [shards(): local = (edge_src - band * 1280).reshape(3, NDEV, CAP)[:, order, :]]
    all_to_all x3 -> x0, starting transfers between devices: 20.4 us -> none  [the longest x1 11.8 us: shards(): lax.all_to_all(send_buffer, ('band', 'sub'), split_axis=0, concat_axis=0,...]
  transfers between devices with their start and end apart: 4 -> 0, of which waited for: 3 -> 0; matrix products, arithmetic and copies ran while one was open for 32% -> 0% of each run, Pallas kernels for 0% -> 0%
where the time goes in v1:
time: 148 us; the launch traced here: 147 us
  Pallas kernels  137 us (93%)
  local copies, waits for them, and re-layouts  8.69 us (6%)
    pallas_call x1, Pallas kernels, shards(): pl.pallas_call(kernel, out_shape=[jax.ShapeDtypeStruct((2, CHIPS, 8, 640)...  135 us
    unnamed x13, local copies, waits for them, and re-layouts  4.18 us

profile of v1, /device:TPU:1, one launch (start us, length us, event | category | flops | bytes accessed | tf_op | source)
XLA Modules:
  0.0 147.4 jit_solution(6491319140611610922)
XLA Ops:
  0.6 0.0 copy-start.5
  0.7 1.3 reshape.429.slot_ref
  2.0 0.8 broadcast_subtract_fusion
  2.8 0.2 reshape.430
  3.0 0.1 copy.17
  3.2 0.8 gather_fusion
  3.9 0.1 reshape.431
  4.1 0.0 copy-done.5
  4.1 0.8 copy.21.w_out_ref
  4.9 0.2 slice.10
  5.2 0.1 transpose_reshape.3
  5.3 0.6 pad.4.index_ref
  6.0 0.0 copy-start
  6.0 0.0 copy-start.1
  6.0 134.8 %shard_map.128 = (bf16[2,64,8,640]{3,2,1,0:T(8,128)(2,1)}, bf16[320,512]{1,0:T(8,128)(2,1)}) custom-call(bf16[227,768]{1,0:T(8,128)(2,1)} %grad_ref.1, bf16[768,512]{1,0:T(8,128)(2,1)} %latent_ref.1, bf16[320,512]{1,0:T(8,128)(2,1)} %mesh_ref.1, s32[1,768]{1,0:T(1,128)} %reshape.429.slot_ref, s32[9,8,256]{2,1,0:T(8,128)} %pad.4.index_ref, ...), custom_call_target="tpu_custom_call" | custom-call | tf_op jit(solution)/shard_map/pallas_call | solution.py:355
  140.8 0.0 copy-done
  140.8 0.0 copy-done.1
  140.8 0.0 copy-start.2
  140.8 1.0 copy-done.2
  141.9 0.0 copy-start.3
  141.9 1.3 copy-done.3
  143.2 0.0 copy-start.4
  143.2 1.0 copy-done.4
  144.2 2.3 %shard_map.129 = (bf16[320,512]{1,0:T(8,128)(2,1)}, f32[512,512]{1,0:T(8,128)}, f32[512,512]{1,0:T(8,128)}, f32[512,512]{1,0:T(8,128)}, f32[512,227]{1,0:T(8,128)S(1)}) custom-call(bf16[2,64,8,640]{3,2,1,0:T(8,128)(2,1)S(1)} %copy-done.3, bf16[320,512]{1,0:T(8,128)(2,1)S(1)} %copy-done.4, bf16[512,512]{1,0:T(8,128)(2,1)S(1)} %copy-done.1, ...), custom_call_target="tpu_custom_call" | custom-call | tf_op jit(solution)/shard_map/pallas_call | solution.py:399
  146.5 1.0 copy.23
  (6 shorter events, 0.1 us)
Async XLA Ops:
  0.6 3.5 %copy-start.5 = (bf16[512,227]{0,1:T(8,128)(2,1)S(1)}, bf16[512,227]{0,1:T(8,128)(2,1)}, u32[]{:S(2)}) copy-start(bf16[512,227]{0,1:T(8,128)(2,1)} %param.17) | copy-start | bytes 697348
  6.0 134.8 %copy-start = (bf16[512,227]{1,0:T(8,128)(2,1)S(1)}, bf16[512,227]{1,0:T(8,128)(2,1)}, u32[]{:S(2)}) copy-start(bf16[512,227]{1,0:T(8,128)(2,1)} %copy.21.w_out_ref) | copy-start | bytes 697348
  6.0 134.8 %copy-start.1 = (bf16[512,512]{1,0:T(8,128)(2,1)S(1)}, bf16[512,512]{1,0:T(8,128)(2,1)}, u32[]{:S(2)}) copy-start(bf16[512,512]{1,0:T(8,128)(2,1)} %w_mesh_ref.3) | copy-start | bytes 1572868
  140.8 1.0 copy-start.2
  141.9 1.3 copy-start.3
  143.2 1.0 copy-start.4

commit v2 on v1

v2 whole, which is shorter than its diff:
```python
import functools
import math

import jax
import jax.numpy as jnp
from jax import lax
from jax.experimental import pallas as pl
from jax.experimental.pallas import tpu as pltpu
from jax.sharding import PartitionSpec as P

MESH = pl.DeviceIdType.MESH
BF, F32 = jnp.bfloat16, jnp.float32
MAIN, OVER = 16, 2
CAP = MAIN + OVER
NDEV = 128
NN = (((1,), (0,)), ((), ()))
NT = (((1,), (1,)), ((), ()))
TN = (((0,), (0,)), ((), ()))
MIX, UNMIX = 13, 5


def dot(a, b, dims):
    return lax.dot_general(a, b, dims, preferred_element_type=F32)


def place():
    band, sub = lax.axis_index("band"), lax.axis_index("sub")
    return lax.div(band, 8), lax.rem(lax.div(band, 2), 4), lax.rem(band, 2), sub


def shifted(u, dy):
    z, x, c, y = place()
    z = lax.rem(z + lax.rem(u, 4), 4)
    x = lax.rem(x + lax.rem(lax.div(u, 4), 4), 4)
    c = lax.rem(c + lax.div(u, 16), 2)
    return z * 8 + x * 2 + c, lax.rem(y + dy, 4)


def near(d):
    return shifted(lax.rem(d * MIX, 32), 0)


def far(d):
    t = d - 32
    q = lax.div(t, 3)
    return shifted(lax.rem(q * MIX, 32), 1 + t - 3 * q)


def source(d):
    z, x, c, y = place()
    t = jnp.maximum(d - 32, 0)
    q = (t * 171) >> 9
    u = jnp.where(d < 32, (d * MIX) & 31, (q * MIX) & 31)
    dy = jnp.where(d < 32, 0, 1 + t - 3 * q)
    band = ((z - u) & 3) * 8 + ((x - (u >> 2)) & 3) * 2 + ((c - (u >> 4)) & 1)
    return band * 4 + ((y - dy) & 3)


ROWS = 256
GROUPS = NDEV * CAP // ROWS
BLOCKS = ROWS // MAIN
CHIPS = 64
SLOTS = NDEV * CAP


def chip_peer(q):
    z, x, c, y = place()
    p = lax.rem(q * 37, CHIPS)
    z = lax.rem(z + lax.div(p, 16), 4)
    x = lax.rem(x + lax.rem(lax.div(p, 4), 4), 4)
    return z * 8 + x * 2 + c, lax.rem(y + lax.rem(p, 4), 4)


def plane_peer(q):
    z, x, c, y = place()
    p = lax.rem(q * 5, 16)
    z = lax.rem(z + lax.div(p, 4), 4)
    x = lax.rem(x + lax.rem(p, 4), 4)
    return (z * 8 + x * 2 + c, y), z * 4 + x


def remote(src, dst, send, recv, device):
    return pltpu.make_async_remote_copy(
        src_ref=src,
        dst_ref=dst,
        send_sem=send,
        recv_sem=recv,
        device_id=device,
        device_id_type=MESH,
    )


def kernel(
    grad_in,
    latent_in,
    mesh_in,
    slot_in,
    edge_in,
    w_mesh_in,
    w_grid_in,
    w_msg_in,
    w_out_in,
    sums_ref,
    proj_ref,
    grad_ref,
    latent_ref,
    slot_ref,
    edge_ref,
    w_mesh_ref,
    w_grid_ref,
    w_msg_ref,
    w_out_ref,
    load_sem,
    index_ref,
    gathered,
    weighted,
    main_send,
    over_send,
    main_recv,
    over_recv,
    patch,
    table,
    back,
    node,
    node_send,
    node_recv,
    rows_ref,
    pre_grad,
    part,
    pair_recv,
    rs_send,
    rs_recv,
    ring_send,
    ring_recv,
    ag_send,
    main_ssem,
    main_rsem,
    ssem,
    rsem,
):
    z, x, c, y = place()
    band = lax.axis_index("band")
    sibling = (band + 1 - 2 * c, y)
    loads = [
        pltpu.make_async_copy(src, dst, load_sem.at[k])
        for k, (src, dst) in enumerate(
            (
                (grad_in, grad_ref),
                (slot_in, slot_ref),
                (latent_in, latent_ref),
                (mesh_in, patch.at[y]),
                (edge_in, edge_ref),
                (w_msg_in, w_msg_ref),
                (w_out_in, w_out_ref),
                (w_mesh_in, w_mesh_ref),
                (w_grid_in, w_grid_ref),
            )
        )
    ]
    for load in loads:
        load.start()
    bar = pltpu.get_barrier_semaphore()

    def each(peer, act):
        def run(d, carry):
            act(d, peer(d))
            return carry

        return run

    def greet(d, device):
        pl.semaphore_signal(bar, inc=1, device_id=device, device_id_type=MESH)

    lax.fori_loop(1, 32, each(near, greet), 0)
    lax.fori_loop(32, NDEV, each(far, greet), 0)
    pl.semaphore_wait(bar, NDEV - 1)
    for k in (1, 2, 3):
        remote(
            mesh_in, patch.at[y], ssem.at[0], rsem.at[0], (band, lax.rem(y + k, 4))
        ).start()

    for load in loads:
        load.wait()
    channels, points = grad_ref.shape
    me = band * 4 + y
    lane = lax.broadcasted_iota(jnp.int32, (1, points), 1)
    total = points * NDEV
    angle = jnp.pi * (((me * points + lane).astype(F32) + 0.5) / total - 0.5)
    weight = 0.5 * jnp.pi * jnp.cos(angle)
    weighted[...] = jnp.zeros_like(weighted)
    weighted[0:channels, :] = (weight * grad_ref[...].astype(F32)).astype(BF)
    slot = slot_ref[...].reshape(1, points)
    j = (slot * 3641) >> 16
    r = slot - j * CAP
    dy = (j - y) & 3
    u = (((j >> 5) - z) & 3) + 4 * (((j >> 3) - x) & 3) + 16 * (((j >> 2) - c) & 1)
    q = (u * UNMIX) & 31
    d = jnp.where(dy == 0, q, 31 + 3 * q + dy)
    at_main = jnp.where(r < MAIN, d * MAIN + r, -1)
    at_over = jnp.where(r >= MAIN, d * OVER + r - MAIN, -1)
    row = lax.broadcasted_iota(jnp.int32, (ROWS, points), 0)

    def pick(at, base):
        hot = jnp.where(row == at - base, 1.0, 0.0).astype(BF)
        lat = dot(hot, latent_ref[...], NN).astype(BF)
        gr = dot(hot, weighted[...], NT).astype(BF)
        return lat, gr

    lat, gr = pick(at_over, 0)
    over_send[:, :, 0:512] = lat.reshape(NDEV, OVER, 512)
    over_send[:, :, 512:768] = gr.reshape(NDEV, OVER, 256)
    over_recv[0] = over_send[0]

    def pick_main(g):
        lat, gr = pick(at_main, g * ROWS)
        blocks = pl.ds(g * BLOCKS, BLOCKS)
        main_send[blocks, :, 0:512] = lat.reshape(BLOCKS, MAIN, 512)
        main_send[blocks, :, 512:768] = gr.reshape(BLOCKS, MAIN, 256)

    def send_over(d, device):
        remote(
            over_send.at[d], over_recv.at[d], ssem.at[1], rsem.at[1], device
        ).start()

    def send_main(d, device):
        remote(
            main_send.at[d],
            main_recv.at[d],
            main_ssem.at[0],
            main_rsem.at[lax.div(d, BLOCKS)],
            device,
        ).start()

    pick_main(0)
    pick_main(1)
    main_recv[0] = main_send[0]
    lax.fori_loop(1, 32, each(near, send_main), 0)
    lax.fori_loop(1, 32, each(near, send_over), 0)

    def prep_group(g, carry):
        pick_main(g)
        return carry

    lax.fori_loop(2, GROUPS - 1, prep_group, 0)
    back[...] = jnp.zeros_like(back)
    back[:, 0:channels] = dot(w_msg_ref[...], w_out_ref[...], NT).astype(BF)
    node[...] = jnp.zeros_like(node)
    part[...] = jnp.zeros_like(part)

    size = table.shape[0]
    local = edge_ref[...] - band * size
    halves = jnp.concatenate(
        [(local >> 4).astype(F32), (local & 15).astype(F32), jnp.zeros((2, SLOTS), F32)], axis=0
    ).astype(BF)
    lanes = lax.broadcasted_iota(jnp.int32, (ROWS, SLOTS), 1)
    line = lax.broadcasted_iota(jnp.int32, (ROWS, 1), 0)

    def find(g, slots):
        hot = jnp.where(lanes == slots, 1.0, 0.0).astype(BF)
        found = dot(halves, hot, NT)
        whole = (found[0:3] * 16.0 + found[3:6]).astype(jnp.int32)
        index_ref[g, 0:3, :] = whole

    def find_main(g, carry):
        find(g, source((g - 1) * BLOCKS + (line >> 4)) * CAP + (line & 15))
        return carry

    index_ref[...] = jnp.zeros_like(index_ref)
    find(0, source(line >> 1) * CAP + MAIN + (line & 1))
    lax.fori_loop(1, GROUPS, find_main, 0)

    remote(
        patch.at[pl.ds(0, 3)], patch.at[pl.ds(0, 3)], ssem.at[0], rsem.at[0], sibling
    ).wait_recv()
    lax.fori_loop(32, NDEV, each(far, send_over), 0)
    lax.fori_loop(32, NDEV, each(far, send_main), 0)
    for k in range(4):
        table[pl.ds(k * 320, 320), :] = dot(patch[k], w_mesh_ref[...], NN).astype(BF)

    def collect(g, carry):
        column = index_ref[g].T
        node_col = lax.broadcasted_iota(jnp.int32, (ROWS, size), 1)
        for k in range(3):
            hot = jnp.where(node_col == column[:, k : k + 1], 1.0, 0.0).astype(BF)
            gathered[g, k] = dot(hot, table[...], NN).astype(BF)
        return carry

    lax.fori_loop(0, GROUPS, collect, 0)

    def group(g):
        latent, grad = rows_ref[:, 0:512], rows_ref[:, 512:768]
        grid_proj = dot(latent, w_grid_ref[...], NN).astype(BF).astype(F32)
        act_grad = dot(grad, back[...], NT)
        index = index_ref[g]
        node_row = lax.broadcasted_iota(jnp.int32, (size, ROWS), 0)
        act = jnp.zeros((ROWS, 512), F32)
        total = jnp.zeros((ROWS, 512), F32)
        for k in range(3):
            pre = gathered[g, k].astype(F32) + grid_proj
            sigma = 0.5 * jnp.tanh(0.5 * pre) + 0.5
            value = pre * sigma
            act += value
            grad_k = (act_grad * (sigma + value * (1.0 - sigma))).astype(BF)
            total += grad_k.astype(F32)
            pre_grad[pl.ds(k * ROWS, ROWS), :] = grad_k
        act = act.astype(BF)
        moment = dot(act, grad, TN)
        part[0, :, 512:640] += moment[:, 0:128]
        part[1, :, 512:640] += moment[:, 128:256]
        part[1, :, 0:512] += dot(latent, total.astype(BF), TN)
        hots = [
            jnp.where(node_row == index[k : k + 1, :], 1.0, 0.0).astype(BF)
            for k in range(3)
        ]
        node[...] += dot(jnp.concatenate(hots, axis=1), pre_grad[...], NN)

    def await_main(g, first, count):
        blocks = pl.ds(first, count)
        remote(
            main_send.at[blocks], main_recv.at[blocks], main_ssem.at[0], main_rsem.at[g], sibling
        ).wait_recv()

    def load_main(g):
        blocks = pl.ds(g * BLOCKS, BLOCKS)
        rows_ref[...] = main_recv[blocks, :, :].reshape(ROWS, 768)

    def step(i, carry):
        @pl.when(i == 0)
        def _():
            await_main(0, 1, BLOCKS - 1)
            load_main(0)

        @pl.when(i == 1)
        def _():
            await_main(1, BLOCKS, BLOCKS)
            load_main(1)

        @pl.when(i == 2)
        def _():
            blocks = pl.ds(1, NDEV - 1)
            remote(
                over_send.at[blocks], over_recv.at[blocks], ssem.at[1], rsem.at[1], sibling
            ).wait_recv()
            rows_ref[...] = over_recv[...].reshape(ROWS, 768)

        @pl.when(i > 2)
        def _():
            await_main(i - 1, (i - 1) * BLOCKS, BLOCKS)
            load_main(i - 1)

        group(jnp.where(i < 2, i + 1, jnp.where(i == 2, 0, i)))
        return carry

    lax.fori_loop(0, GROUPS, step, 0)

    def node_copy(k):
        to = (y + k) % 4
        return remote(
            node_send.at[to], node_recv.at[k - 1], ssem.at[2], rsem.at[2], (band, to)
        )

    for k in range(4):
        node_send[k] = node[pl.ds(k * 320, 320), :].astype(BF)
    for k in (1, 2, 3):
        node_copy(k).start()
    mesh_part = dot(patch[0], node_send[0], TN)
    for k in (1, 2, 3):
        mesh_part += dot(patch[k], node_send[k], TN)
    part[0, :, 0:512] = mesh_part
    pair = remote(part.at[1 - c], pair_recv, ssem.at[3], rsem.at[3], sibling)
    pair.start()
    pair.wait_recv()
    rs_send[...] = (part[c] + pair_recv[...]).astype(BF).reshape(16, 32, 640)

    def scatter(q, carry):
        device, plane = plane_peer(q)
        remote(rs_send.at[plane], rs_recv.at[q], ssem.at[4], rsem.at[4], device).start()
        return carry

    lax.fori_loop(1, 16, scatter, 0)
    plane = z * 4 + x
    rs_recv[0] = rs_send[plane]
    others = pl.ds(1, 15)
    scattered = remote(
        rs_send.at[others], rs_recv.at[others], ssem.at[4], rsem.at[4], sibling
    )
    scattered.wait_recv()
    plane_sum = rs_recv[0].astype(F32)
    for k in range(1, 16):
        plane_sum += rs_recv[k].astype(F32)
    ring_send[...] = plane_sum.astype(BF).reshape(4, 8, 640)
    for k in (1, 2, 3):
        to = lax.rem(y + k, 4)
        remote(
            ring_send.at[to], ring_recv.at[k - 1], ssem.at[7], rsem.at[7], (band, to)
        ).start()
    ring = remote(
        ring_send.at[pl.ds(0, 3)], ring_recv, ssem.at[7], rsem.at[7], sibling
    )
    ring.wait_recv()
    full = ring_send[y].astype(F32)
    for k in range(3):
        full += ring_recv[k].astype(F32)
    chip = plane * 4 + y
    scale = 1.0 / math.sqrt(3.0 * points * NDEV)
    ag_send[...] = (full * scale).astype(BF)
    sums_ref[c, chip] = ag_send[...]

    def gather(q, carry):
        remote(
            ag_send, sums_ref.at[c, chip], ssem.at[5], rsem.at[5], chip_peer(q)
        ).start()
        return carry

    lax.fori_loop(1, CHIPS, gather, 0)

    remote(
        node_send.at[pl.ds(0, 3)], node_recv, ssem.at[2], rsem.at[2], sibling
    ).wait_recv()
    mine = node[pl.ds(y * 320, 320), :]
    proj_ref[...] = (
        mine + node_recv[0].astype(F32) + node_recv[1].astype(F32) + node_recv[2].astype(F32)
    ).astype(BF)

    most = sums_ref.at[c, pl.ds(0, CHIPS - 1)]
    remote(most, most, ssem.at[5], rsem.at[5], sibling).wait_recv()
    share = remote(sums_ref.at[c], sums_ref.at[c], ssem.at[6], rsem.at[6], sibling)
    share.start()

    three = node_send.at[pl.ds(0, 3)]
    remote(patch.at[pl.ds(0, 3)], patch.at[pl.ds(0, 3)], ssem.at[0], rsem.at[0], sibling).wait_send()
    blocks = pl.ds(1, NDEV - 1)
    remote(over_send.at[blocks], over_recv.at[blocks], ssem.at[1], rsem.at[1], sibling).wait_send()
    remote(main_send.at[blocks], main_recv.at[blocks], main_ssem.at[0], main_rsem.at[0], sibling).wait_send()
    remote(three, node_recv, ssem.at[2], rsem.at[2], sibling).wait_send()
    pair.wait_send()
    scattered.wait_send()
    ring.wait_send()
    remote(most, most, ssem.at[5], rsem.at[5], sibling).wait_send()
    share.wait()


def final_kernel(
    sums_in,
    proj_in,
    w_mesh_in,
    w_msg_in,
    w_out_in,
    node_ref,
    mesh_ref,
    grid_ref,
    msg_ref,
    out_ref,
    sums_ref,
    proj_ref,
    w_mesh_ref,
    w_msg_ref,
    w_out_ref,
    load_sem,
):
    loads = [
        pltpu.make_async_copy(src, dst, load_sem.at[k])
        for k, (src, dst) in enumerate(
            (
                (sums_in, sums_ref),
                (proj_in, proj_ref),
                (w_mesh_in, w_mesh_ref),
                (w_msg_in, w_msg_ref),
                (w_out_in, w_out_ref),
            )
        )
    ]
    for load in loads:
        load.start()
    for load in loads:
        load.wait()
    node_ref[...] = dot(proj_ref[...], w_mesh_ref[...], NT).astype(BF)
    mesh_ref[...] = sums_ref[0, :, :, 0:512].astype(F32).reshape(512, 512)
    grid_ref[...] = sums_ref[1, :, :, 0:512].astype(F32).reshape(512, 512)
    low = sums_ref[0, :, :, 512:640].astype(F32).reshape(512, 128)
    high = sums_ref[1, :, :, 512:640].astype(F32).reshape(512, 128)
    moment = jnp.concatenate([low, high], axis=1)[:, 0:227].astype(BF)
    msg_ref[...] = dot(moment, w_out_ref[...], NN)
    out_ref[...] = dot(moment, w_msg_ref[...], TN)


def shards(grad_pred, grid_latent, mesh_latent, send_slot, edge_src, w_mesh, w_grid, w_msg, w_out):
    vmem = pltpu.VMEM
    w_out = w_out.T
    hbm = pl.BlockSpec(memory_space=pltpu.HBM)
    sums, proj = pl.pallas_call(
        kernel,
        in_specs=[hbm] * 9,
        out_shape=[
            jax.ShapeDtypeStruct((2, CHIPS, 8, 640), BF),
            jax.ShapeDtypeStruct((320, 512), BF),
        ],
        scratch_shapes=[
            vmem((227, 768), BF),
            vmem((768, 512), BF),
            vmem((768,), jnp.int32),
            vmem((3, SLOTS), jnp.int32),
            vmem((512, 512), BF),
            vmem((512, 512), BF),
            vmem((512, 512), BF),
            vmem((227, 512), BF),
            pltpu.SemaphoreType.DMA((9,)),
            vmem((GROUPS, 8, ROWS), jnp.int32),
            vmem((GROUPS, 3, ROWS, 512), BF),
            vmem((256, 768), BF),
            vmem((NDEV, MAIN, 768), BF),
            vmem((NDEV, OVER, 768), BF),
            vmem((NDEV, MAIN, 768), BF),
            vmem((NDEV, OVER, 768), BF),
            vmem((4, 320, 512), BF),
            vmem((1280, 512), BF),
            vmem((512, 256), BF),
            vmem((1280, 512), F32),
            vmem((4, 320, 512), BF),
            vmem((3, 320, 512), BF),
            vmem((ROWS, 768), BF),
            vmem((3 * ROWS, 512), BF),
            vmem((2, 512, 640), F32),
            vmem((512, 640), F32),
            vmem((16, 32, 640), BF),
            vmem((16, 32, 640), BF),
            vmem((4, 8, 640), BF),
            vmem((3, 8, 640), BF),
            vmem((8, 640), BF),
            pltpu.SemaphoreType.DMA((1,)),
            pltpu.SemaphoreType.DMA((GROUPS - 1,)),
            pltpu.SemaphoreType.DMA((8,)),
            pltpu.SemaphoreType.DMA((8,)),
        ],
        compiler_params=pltpu.CompilerParams(
            collective_id=0, has_side_effects=True, vmem_limit_bytes=67_043_328
        ),
    )(grad_pred, grid_latent, mesh_latent, send_slot, edge_src, w_mesh, w_grid, w_msg, w_out)
    *grads, out_grad = pl.pallas_call(
        final_kernel,
        out_shape=[
            jax.ShapeDtypeStruct((320, 512), BF),
            jax.ShapeDtypeStruct((512, 512), F32),
            jax.ShapeDtypeStruct((512, 512), F32),
            jax.ShapeDtypeStruct((512, 512), F32),
            jax.ShapeDtypeStruct((227, 512), F32),
        ],
        in_specs=[hbm] * 5,
        scratch_shapes=[
            vmem((2, CHIPS, 8, 640), BF),
            vmem((320, 512), BF),
            vmem((512, 512), BF),
            vmem((512, 512), BF),
            vmem((227, 512), BF),
            pltpu.SemaphoreType.DMA((5,)),
        ],
        compiler_params=pltpu.CompilerParams(vmem_limit_bytes=67_043_328),
    )(sums, proj, w_mesh, w_msg, w_out)
    return *grads, out_grad.T


def solution(mesh):
    both = ("band", "sub")
    placed = (P(None, both), P(both, None), P(both, None), P(both), P(None, both))
    return jax.shard_map(
        shards,
        mesh=mesh,
        in_specs=placed + (P(),) * 4,
        out_specs=(P(both, None), P(), P(), P(), P()),
        check_vma=False,
    )
```

time: 148 us -> 117 us (0.79)
  Pallas kernels: 137 us -> 116 us
  local copies, waits for them, and re-layouts: 8.69 us -> 0 us
    pallas_call x1, Pallas kernels: 135 us -> 112 us  [shards(): pl.pallas_call(kernel, in_specs=[hbm] * 9, out_shape=[jax.ShapeDtypeStruc...]
    unnamed x13 -> x0, local copies, waits for them, and re-layouts: 4.18 us -> none
    pallas_call x1, Pallas kernels: 2.3 us -> 4.21 us  [shards(): pl.pallas_call(final_kernel, out_shape=[jax.ShapeDtypeStruct((320, 512),...]
    reshape x5 -> x0, local copies, waits for them, and re-layouts: 1.78 us -> none  [the longest x1 1.3 us: shards(): send_slot.reshape(1, -1)]
where the time goes in v2:
time: 117 us
  Pallas kernels  116 us (99%)
    pallas_call x1, Pallas kernels, shards(): pl.pallas_call(kernel, in_specs=[hbm] * 9, out_shape=[jax.ShapeDtypeStruc...  112 us
    pallas_call x1, Pallas kernels, shards(): pl.pallas_call(final_kernel, out_shape=[jax.ShapeDtypeStruct((320, 512),...  4.21 us

profile of v2, /device:TPU:1, one launch (start us, length us, event | category | flops | bytes accessed | tf_op | source)
XLA Modules:
  0.0 116.9 jit_solution(15379085223898861814)
XLA Ops:
  0.6 112.1 %shard_map.128 = (bf16[2,64,8,640]{3,2,1,0:T(8,128)(2,1)}, bf16[320,512]{1,0:T(8,128)(2,1)}) custom-call(bf16[227,768]{1,0:T(8,128)(2,1)} %grad_in.1, bf16[768,512]{1,0:T(8,128)(2,1)} %latent_in.1, bf16[320,512]{1,0:T(8,128)(2,1)} %mesh_in.1, s32[768]{0:T(1024)} %slot_in.1, s32[3,2304]{1,0:T(4,128)} %edge_in.1, bf16[512,512]{1,0:T(8,128)(2,1)} %w_mesh_in.3, ...), custom_call_target="tpu_custom_call" | custom-call | tf_op jit(solution)/shard_map/pallas_call | solution.py:491
  112.7 4.2 %shard_map.129 = (bf16[320,512]{1,0:T(8,128)(2,1)}, f32[512,512]{1,0:T(8,128)}, f32[512,512]{1,0:T(8,128)}, f32[512,512]{1,0:T(8,128)}, f32[227,512]{1,0:T(8,128)}) custom-call(bf16[2,64,8,640]{3,2,1,0:T(8,128)(2,1)} %get-tuple-element.12.sums_in, bf16[320,512]{1,0:T(8,128)(2,1)} %get-tuple-element.13.proj_in, bf16[512,512]{1,0:T(8,128)(2,1)} %w_mesh_in.3, ...), custom_call_target="tpu_custom_call" | custom-call | tf_op jit(solution)/shard_map/pallas_call | solution.py:539

commit v3 on v2

v3 whole, which is shorter than its diff:
```python
import functools
import math

import jax
import jax.numpy as jnp
from jax import lax
from jax.experimental import pallas as pl
from jax.experimental.pallas import tpu as pltpu
from jax.sharding import PartitionSpec as P

MESH = pl.DeviceIdType.MESH
BF, F32 = jnp.bfloat16, jnp.float32
MAIN, OVER = 16, 2
CAP = MAIN + OVER
NDEV = 128
NN = (((1,), (0,)), ((), ()))
NT = (((1,), (1,)), ((), ()))
TN = (((0,), (0,)), ((), ()))
MIX, UNMIX = 13, 5


def dot(a, b, dims):
    return lax.dot_general(a, b, dims, preferred_element_type=F32)


def place():
    band, sub = lax.axis_index("band"), lax.axis_index("sub")
    return lax.div(band, 8), lax.rem(lax.div(band, 2), 4), lax.rem(band, 2), sub


def shifted(u, dy):
    z, x, c, y = place()
    z = lax.rem(z + lax.rem(u, 4), 4)
    x = lax.rem(x + lax.rem(lax.div(u, 4), 4), 4)
    c = lax.rem(c + lax.div(u, 16), 2)
    return z * 8 + x * 2 + c, lax.rem(y + dy, 4)


def near(d):
    return shifted(lax.rem(d * MIX, 32), 0)


def beside(d):
    t = d - 32
    return shifted(lax.rem(lax.div(t, 2) * MIX, 32), 1 + 2 * lax.rem(t, 2))


def opposite(d):
    return shifted(lax.rem((d - 96) * MIX, 32), 2)


def source(d):
    z, x, c, y = place()
    q = jnp.where(d < 32, d, jnp.where(d < 96, (d - 32) >> 1, d - 96))
    u = (q * MIX) & 31
    dy = jnp.where(d < 32, 0, jnp.where(d < 96, 1 + 2 * (d & 1), 2))
    band = ((z - u) & 3) * 8 + ((x - (u >> 2)) & 3) * 2 + ((c - (u >> 4)) & 1)
    return band * 4 + ((y - dy) & 3)


ROWS = 256
GROUPS = NDEV * CAP // ROWS
BLOCKS = ROWS // MAIN
SLOTS = NDEV * CAP


def plane_peer(q):
    z, x, c, y = place()
    p = lax.rem(q * 5, 16)
    z = lax.rem(z + lax.div(p, 4), 4)
    x = lax.rem(x + lax.rem(p, 4), 4)
    return (z * 8 + x * 2 + c, y), z * 4 + x


def remote(src, dst, send, recv, device):
    return pltpu.make_async_remote_copy(
        src_ref=src,
        dst_ref=dst,
        send_sem=send,
        recv_sem=recv,
        device_id=device,
        device_id_type=MESH,
    )


def kernel(
    grad_in,
    latent_in,
    mesh_in,
    slot_in,
    edge_in,
    w_mesh_in,
    w_grid_in,
    w_msg_in,
    w_out_in,
    outer_ref,
    inner_ref,
    proj_ref,
    grad_ref,
    latent_ref,
    slot_ref,
    edge_ref,
    w_mesh_ref,
    w_grid_ref,
    w_msg_ref,
    w_out_ref,
    load_sem,
    index_ref,
    gathered,
    weighted,
    main_send,
    over_send,
    main_recv,
    over_recv,
    patch,
    table,
    back,
    node,
    node_send,
    node_recv,
    rows_ref,
    outer_part,
    outer_pair,
    outer_rs_send,
    outer_rs_recv,
    outer_ring_send,
    outer_ring_recv,
    inner_part,
    inner_pair,
    inner_rs_send,
    inner_rs_recv,
    inner_ring_send,
    inner_ring_recv,
    psem,
    qsem,
    main_ssem,
    main_rsem,
    ssem,
    rsem,
):
    z, x, c, y = place()
    band = lax.axis_index("band")
    sibling = (band + 1 - 2 * c, y)
    loads = [
        pltpu.make_async_copy(src, dst, load_sem.at[k])
        for k, (src, dst) in enumerate(
            (
                (grad_in, grad_ref),
                (slot_in, slot_ref),
                (latent_in, latent_ref),
                (mesh_in, patch.at[y]),
                (edge_in, edge_ref),
                (w_msg_in, w_msg_ref),
                (w_out_in, w_out_ref),
                (w_mesh_in, w_mesh_ref),
                (w_grid_in, w_grid_ref),
            )
        )
    ]
    for load in loads:
        load.start()
    bar = pltpu.get_barrier_semaphore()

    def each(peer, act):
        def run(d, carry):
            act(d, peer(d))
            return carry

        return run

    def greet(d, device):
        pl.semaphore_signal(bar, inc=1, device_id=device, device_id_type=MESH)

    lax.fori_loop(1, 32, each(near, greet), 0)
    lax.fori_loop(32, 96, each(beside, greet), 0)
    lax.fori_loop(96, NDEV, each(opposite, greet), 0)
    loads[3].wait()
    pl.semaphore_wait(bar, NDEV - 1)
    above, below = lax.rem(y + 1, 4), lax.rem(y + 3, 4)
    half = pl.ds(0, 160)
    rest = pl.ds(160, 160)

    def patch_copy(n, block, to):
        return remote(block, block, psem.at[n], qsem.at[n], (band, to))

    up = patch_copy(0, patch.at[y], above)
    down = patch_copy(1, patch.at[y], below)
    up_half = patch_copy(2, patch.at[below, rest], above)
    down_half = patch_copy(3, patch.at[above, half], below)
    up.start()
    down.start()
    for k in (0, 1, 2, 4, 5, 6, 7, 8):
        loads[k].wait()
    channels, points = grad_ref.shape
    me = band * 4 + y
    lane = lax.broadcasted_iota(jnp.int32, (1, points), 1)
    total = points * NDEV
    angle = jnp.pi * (((me * points + lane).astype(F32) + 0.5) / total - 0.5)
    weight = 0.5 * jnp.pi * jnp.cos(angle)
    weighted[...] = jnp.zeros_like(weighted)
    weighted[0:channels, :] = (weight * grad_ref[...].astype(F32)).astype(BF)
    slot = slot_ref[...].reshape(1, points)
    j = (slot * 3641) >> 16
    r = slot - j * CAP
    dy = (j - y) & 3
    u = (((j >> 5) - z) & 3) + 4 * (((j >> 3) - x) & 3) + 16 * (((j >> 2) - c) & 1)
    q = (u * UNMIX) & 31
    d = jnp.where(dy == 0, q, jnp.where(dy == 2, 96 + q, 32 + 2 * q + (dy >> 1)))
    at_main = jnp.where(r < MAIN, d * MAIN + r, -1)
    at_over = jnp.where(r >= MAIN, d * OVER + r - MAIN, -1)
    row = lax.broadcasted_iota(jnp.int32, (ROWS, points), 0)

    def pick(at, base):
        hot = jnp.where(row == at - base, 1.0, 0.0).astype(BF)
        lat = dot(hot, latent_ref[...], NN).astype(BF)
        gr = dot(hot, weighted[...], NT).astype(BF)
        return lat, gr

    lat, gr = pick(at_over, 0)
    over_send[:, :, 0:512] = lat.reshape(NDEV, OVER, 512)
    over_send[:, :, 512:768] = gr.reshape(NDEV, OVER, 256)
    over_recv[0] = over_send[0]

    def pick_main(g):
        lat, gr = pick(at_main, g * ROWS)
        blocks = pl.ds(g * BLOCKS, BLOCKS)
        main_send[blocks, :, 0:512] = lat.reshape(BLOCKS, MAIN, 512)
        main_send[blocks, :, 512:768] = gr.reshape(BLOCKS, MAIN, 256)

    def send_over(d, device):
        remote(
            over_send.at[d], over_recv.at[d], ssem.at[1], rsem.at[1], device
        ).start()

    def send_main(d, device):
        remote(
            main_send.at[d],
            main_recv.at[d],
            main_ssem.at[0],
            main_rsem.at[lax.div(d, BLOCKS)],
            device,
        ).start()

    pick_main(0)
    pick_main(1)
    main_recv[0] = main_send[0]
    lax.fori_loop(1, 32, each(near, send_main), 0)
    lax.fori_loop(1, 32, each(near, send_over), 0)

    def prep_group(g, carry):
        pick_main(g)
        return carry

    lax.fori_loop(2, GROUPS - 1, prep_group, 0)
    up.wait_recv()
    up_half.start()
    down.wait_recv()
    down_half.start()
    back[...] = jnp.zeros_like(back)
    back[:, 0:channels] = dot(w_msg_ref[...], w_out_ref[...], NT).astype(BF)
    node[...] = jnp.zeros_like(node)
    outer_part[...] = jnp.zeros_like(outer_part)

    size = table.shape[0]
    local = edge_ref[...] - band * size
    halves = jnp.concatenate(
        [(local >> 4).astype(F32), (local & 15).astype(F32), jnp.zeros((2, SLOTS), F32)], axis=0
    ).astype(BF)
    lanes = lax.broadcasted_iota(jnp.int32, (ROWS, SLOTS), 1)
    line = lax.broadcasted_iota(jnp.int32, (ROWS, 1), 0)

    def find(g, slots):
        hot = jnp.where(lanes == slots, 1.0, 0.0).astype(BF)
        found = dot(halves, hot, NT)
        whole = (found[0:3] * 16.0 + found[3:6]).astype(jnp.int32)
        index_ref[g, 0:3, :] = whole

    def find_main(g, carry):
        find(g, source((g - 1) * BLOCKS + (line >> 4)) * CAP + (line & 15))
        return carry

    index_ref[...] = jnp.zeros_like(index_ref)
    find(0, source(line >> 1) * CAP + MAIN + (line & 1))
    lax.fori_loop(1, GROUPS, find_main, 0)

    up_half.wait_recv()
    down_half.wait_recv()
    lax.fori_loop(32, 96, each(beside, send_over), 0)
    lax.fori_loop(96, NDEV, each(opposite, send_over), 0)
    lax.fori_loop(32, 96, each(beside, send_main), 0)
    lax.fori_loop(96, NDEV, each(opposite, send_main), 0)
    for k in range(4):
        table[pl.ds(k * 320, 320), :] = dot(patch[k], w_mesh_ref[...], NN).astype(BF)

    def collect(g, carry):
        column = index_ref[g].T
        node_col = lax.broadcasted_iota(jnp.int32, (ROWS, size), 1)
        for k in range(3):
            hot = jnp.where(node_col == column[:, k : k + 1], 1.0, 0.0).astype(BF)
            gathered[g, k] = dot(hot, table[...], NN).astype(BF)
        return carry

    lax.fori_loop(0, GROUPS, collect, 0)

    def group(g):
        latent, grad = rows_ref[:, 0:512], rows_ref[:, 512:768]
        grid_proj = dot(latent, w_grid_ref[...], NN).astype(BF).astype(F32)
        act_grad = dot(grad, back[...], NT)
        act = jnp.zeros((ROWS, 512), F32)
        total = jnp.zeros((ROWS, 512), F32)
        for k in range(3):
            pre = gathered[g, k].astype(F32) + grid_proj
            sigma = 0.5 * jnp.tanh(0.5 * pre) + 0.5
            value = pre * sigma
            act += value
            grad_k = (act_grad * (sigma + value * (1.0 - sigma))).astype(BF)
            total += grad_k.astype(F32)
            gathered[g, k] = grad_k
        act = act.astype(BF)
        moment = dot(act, grad, TN)
        across = dot(latent, total.astype(BF), TN)
        for h in range(2):
            outer_part[h, :, 0:256] += across[:, h * 256 : h * 256 + 256]
            outer_part[h, :, 256:384] += moment[:, h * 128 : h * 128 + 128]

    def spread(g):
        index = index_ref[g]
        node_row = lax.broadcasted_iota(jnp.int32, (size, ROWS), 0)
        hots = [
            jnp.where(node_row == index[k : k + 1, :], 1.0, 0.0).astype(BF)
            for k in range(3)
        ]
        values = gathered[g].reshape(3 * ROWS, 512)
        node[...] += dot(jnp.concatenate(hots, axis=1), values, NN)

    def await_main(g, first, count):
        blocks = pl.ds(first, count)
        remote(
            main_send.at[blocks], main_recv.at[blocks], main_ssem.at[0], main_rsem.at[g], sibling
        ).wait_recv()

    def load_main(g):
        blocks = pl.ds(g * BLOCKS, BLOCKS)
        rows_ref[...] = main_recv[blocks, :, :].reshape(ROWS, 768)

    def turn(i):
        return jnp.where(i < 2, i + 1, jnp.where(i == 2, 0, i))

    def step(i, carry):
        @pl.when(i > 0)
        def _():
            spread(turn(i - 1))

        @pl.when(i == 0)
        def _():
            await_main(0, 1, BLOCKS - 1)
            load_main(0)

        @pl.when(i == 1)
        def _():
            await_main(1, BLOCKS, BLOCKS)
            load_main(1)

        @pl.when(i == 2)
        def _():
            blocks = pl.ds(1, NDEV - 1)
            remote(
                over_send.at[blocks], over_recv.at[blocks], ssem.at[1], rsem.at[1], sibling
            ).wait_recv()
            rows_ref[...] = over_recv[...].reshape(ROWS, 768)

        @pl.when(i > 2)
        def _():
            await_main(i - 1, (i - 1) * BLOCKS, BLOCKS)
            load_main(i - 1)

        group(turn(i))
        return carry

    lax.fori_loop(0, GROUPS, step, 0)

    plane = z * 4 + x
    scale = 1.0 / math.sqrt(3.0 * points * NDEV)

    def chain(base, part, pair_recv, rs_send, rs_recv, ring_send, ring_recv, sums):
        width = part.shape[2]

        def lane(n):
            return ssem.at[base + n], rsem.at[base + n]

        pair = remote(part.at[1 - c], pair_recv, *lane(0), sibling)
        others = pl.ds(1, 15)
        scattered = remote(rs_send.at[others], rs_recv.at[others], *lane(1), sibling)
        three = ring_send.at[pl.ds(0, 3)]
        ringed = remote(three, ring_recv, *lane(2), sibling)
        lifted = sums.at[c, plane, pl.ds(0, 3)]
        lifted = remote(lifted, lifted, *lane(3), sibling)
        most = sums.at[c, pl.ds(0, 15)]
        spread_out = remote(most, most, *lane(4), sibling)
        share = remote(sums.at[c], sums.at[c], *lane(5), sibling)

        def scatter():
            pair.wait_recv()
            rs_send[...] = (part[c] + pair_recv[...]).astype(BF).reshape(16, 32, width)

            def send(q, carry):
                device, to = plane_peer(q)
                remote(rs_send.at[to], rs_recv.at[q], *lane(1), device).start()
                return carry

            lax.fori_loop(1, 16, send, 0)
            rs_recv[0] = rs_send[plane]

        def ring():
            scattered.wait_recv()
            whole = rs_recv[0].astype(F32)
            for k in range(1, 16):
                whole += rs_recv[k].astype(F32)
            ring_send[...] = whole.astype(BF).reshape(4, 8, width)
            for k in (1, 2, 3):
                to = lax.rem(y + k, 4)
                remote(ring_send.at[to], ring_recv.at[k - 1], *lane(2), (band, to)).start()

        def lift():
            ringed.wait_recv()
            whole = ring_send[y].astype(F32)
            for k in range(3):
                whole += ring_recv[k].astype(F32)
            sums[c, plane, y] = (whole * scale).astype(BF)
            block = sums.at[c, plane, y]
            for k in (1, 2, 3):
                remote(block, block, *lane(3), (band, lax.rem(y + k, 4))).start()

        def gather():
            lifted.wait_recv()
            block = sums.at[c, plane]

            def send(q, carry):
                device, _ = plane_peer(q)
                remote(block, block, *lane(4), device).start()
                return carry

            lax.fori_loop(1, 16, send, 0)

        def swap():
            spread_out.wait_recv()
            share.start()

        def drain():
            for copy in (pair, scattered, ringed, lifted, spread_out):
                copy.wait_send()
            share.wait()

        return pair, scatter, ring, lift, gather, swap, drain

    a_pair, a_scatter, a_ring, a_lift, a_gather, a_swap, a_drain = chain(
        4, outer_part, outer_pair, outer_rs_send, outer_rs_recv, outer_ring_send, outer_ring_recv, outer_ref
    )
    b_pair, b_scatter, b_ring, b_lift, b_gather, b_swap, b_drain = chain(
        10, inner_part, inner_pair, inner_rs_send, inner_rs_recv, inner_ring_send, inner_ring_recv, inner_ref
    )

    def node_send_half(n, rows):
        for k in (1, 2, 3):
            to = lax.rem(y + k, 4)
            remote(
                node_send.at[to, rows], node_recv.at[k - 1, rows], ssem.at[n], rsem.at[n], (band, to)
            ).start()

    def node_wait(n, rows):
        return remote(
            node_send.at[pl.ds(0, 3), rows], node_recv.at[:, rows], ssem.at[n], rsem.at[n], sibling
        )

    a_pair.start()
    spread(GROUPS - 1)
    for k in range(4):
        node_send[k] = node[pl.ds(k * 320, 320), :].astype(BF)
    a_scatter()
    node_send_half(2, half)
    across = dot(patch[0], node_send[0], TN)
    for k in (1, 2, 3):
        across += dot(patch[k], node_send[k], TN)
    for h in range(2):
        inner_part[h] = across[:, h * 256 : h * 256 + 256]
    b_pair.start()
    b_scatter()
    a_ring()
    b_ring()
    a_lift()
    b_lift()
    node_send_half(3, rest)
    a_gather()
    b_gather()
    first, second = node_wait(2, half), node_wait(3, rest)
    first.wait_recv()
    second.wait_recv()
    mine = node[pl.ds(y * 320, 320), :]
    proj_ref[...] = (
        mine + node_recv[0].astype(F32) + node_recv[1].astype(F32) + node_recv[2].astype(F32)
    ).astype(BF)
    a_swap()
    b_swap()

    for copy in (up, down, up_half, down_half, first, second):
        copy.wait_send()
    blocks = pl.ds(1, NDEV - 1)
    remote(over_send.at[blocks], over_recv.at[blocks], ssem.at[1], rsem.at[1], sibling).wait_send()
    remote(main_send.at[blocks], main_recv.at[blocks], main_ssem.at[0], main_rsem.at[0], sibling).wait_send()
    a_drain()
    b_drain()


def final_kernel(*refs):
    ins, outs, held, done, sems = refs[0:6], refs[6:11], refs[11:17], refs[17:22], refs[22]
    loads = [
        pltpu.make_async_copy(src, dst, sems.at[k])
        for k, (src, dst) in enumerate(zip(ins, held))
    ]
    for load in loads:
        load.start()
    stores = [
        pltpu.make_async_copy(src, dst, sems.at[6 + k])
        for k, (src, dst) in enumerate(zip(done, outs))
    ]
    outer_ref, inner_ref, proj_ref, w_mesh_ref, w_msg_ref, w_out_ref = held
    node_ref, mesh_ref, grid_ref, msg_ref, out_ref = done
    loads[1].wait()
    for h in range(2):
        mesh_ref[:, h * 256 : h * 256 + 256] = inner_ref[h].astype(F32).reshape(512, 256)
    stores[1].start()
    loads[0].wait()
    moment = []
    for h in range(2):
        whole = outer_ref[h].astype(F32).reshape(512, 384)
        grid_ref[:, h * 256 : h * 256 + 256] = whole[:, 0:256]
        moment.append(whole[:, 256:384])
    stores[2].start()
    moment = jnp.concatenate(moment, axis=1)[:, 0:227].astype(BF)
    loads[5].wait()
    msg_ref[...] = dot(moment, w_out_ref[...], NN)
    stores[3].start()
    loads[4].wait()
    out_ref[...] = dot(moment, w_msg_ref[...], TN)
    stores[4].start()
    loads[2].wait()
    loads[3].wait()
    node_ref[...] = dot(proj_ref[...], w_mesh_ref[...], NT).astype(BF)
    stores[0].start()
    for store in stores:
        store.wait()


def shards(grad_pred, grid_latent, mesh_latent, send_slot, edge_src, w_mesh, w_grid, w_msg, w_out):
    vmem = pltpu.VMEM
    w_out = w_out.T
    hbm = pl.BlockSpec(memory_space=pltpu.HBM)
    outer, inner, proj = pl.pallas_call(
        kernel,
        in_specs=[hbm] * 9,
        out_shape=[
            jax.ShapeDtypeStruct((2, 16, 4, 8, 384), BF),
            jax.ShapeDtypeStruct((2, 16, 4, 8, 256), BF),
            jax.ShapeDtypeStruct((320, 512), BF),
        ],
        scratch_shapes=[
            vmem((227, 768), BF),
            vmem((768, 512), BF),
            vmem((768,), jnp.int32),
            vmem((3, SLOTS), jnp.int32),
            vmem((512, 512), BF),
            vmem((512, 512), BF),
            vmem((512, 512), BF),
            vmem((227, 512), BF),
            pltpu.SemaphoreType.DMA((9,)),
            vmem((GROUPS, 8, ROWS), jnp.int32),
            vmem((GROUPS, 3, ROWS, 512), BF),
            vmem((256, 768), BF),
            vmem((NDEV, MAIN, 768), BF),
            vmem((NDEV, OVER, 768), BF),
            vmem((NDEV, MAIN, 768), BF),
            vmem((NDEV, OVER, 768), BF),
            vmem((4, 320, 512), BF),
            vmem((1280, 512), BF),
            vmem((512, 256), BF),
            vmem((1280, 512), F32),
            vmem((4, 320, 512), BF),
            vmem((3, 320, 512), BF),
            vmem((ROWS, 768), BF),
            vmem((2, 512, 384), F32),
            vmem((512, 384), F32),
            vmem((16, 32, 384), BF),
            vmem((16, 32, 384), BF),
            vmem((4, 8, 384), BF),
            vmem((3, 8, 384), BF),
            vmem((2, 512, 256), F32),
            vmem((512, 256), F32),
            vmem((16, 32, 256), BF),
            vmem((16, 32, 256), BF),
            vmem((4, 8, 256), BF),
            vmem((3, 8, 256), BF),
            pltpu.SemaphoreType.DMA((4,)),
            pltpu.SemaphoreType.DMA((4,)),
            pltpu.SemaphoreType.DMA((1,)),
            pltpu.SemaphoreType.DMA((GROUPS - 1,)),
            pltpu.SemaphoreType.DMA((16,)),
            pltpu.SemaphoreType.DMA((16,)),
        ],
        compiler_params=pltpu.CompilerParams(
            collective_id=0, has_side_effects=True, vmem_limit_bytes=67_043_328
        ),
    )(grad_pred, grid_latent, mesh_latent, send_slot, edge_src, w_mesh, w_grid, w_msg, w_out)
    shapes = [
        ((320, 512), BF),
        ((512, 512), F32),
        ((512, 512), F32),
        ((512, 512), F32),
        ((227, 512), F32),
    ]
    operands = (outer, inner, proj, w_mesh, w_msg, w_out)
    *grads, out_grad = pl.pallas_call(
        final_kernel,
        out_shape=[jax.ShapeDtypeStruct(*shape) for shape in shapes],
        in_specs=[hbm] * 6,
        out_specs=[hbm] * 5,
        scratch_shapes=[
            *(vmem(operand.shape, BF) for operand in operands),
            *(vmem(*shape) for shape in shapes),
            pltpu.SemaphoreType.DMA((11,)),
        ],
        compiler_params=pltpu.CompilerParams(vmem_limit_bytes=67_043_328),
    )(*operands)
    return *grads, out_grad.T


def solution(mesh):
    both = ("band", "sub")
    placed = (P(None, both), P(both, None), P(both, None), P(both), P(None, both))
    return jax.shard_map(
        shards,
        mesh=mesh,
        in_specs=placed + (P(),) * 4,
        out_specs=(P(both, None), P(), P(), P(), P()),
        check_vma=False,
    )
```

time: 117 us -> 110 us (0.940)
  Pallas kernels: 116 us -> 110 us
    pallas_call x1, Pallas kernels: 112 us -> 106 us  [shards(): pl.pallas_call(kernel, in_specs=[hbm] * 9, out_shape=[jax.ShapeDtypeStruc...]
where the time goes in v3:
time: 110 us
  Pallas kernels  110 us (100%)
    pallas_call x1, Pallas kernels, shards(): pl.pallas_call(kernel, in_specs=[hbm] * 9, out_shape=[jax.ShapeDtypeStruc...  106 us
    pallas_call x1, Pallas kernels, shards(): pl.pallas_call(final_kernel, out_shape=[jax.ShapeDtypeStruct(*shape) for...  3.55 us

profile of v3, /device:TPU:1, one launch (start us, length us, event | category | flops | bytes accessed | tf_op | source)
XLA Modules:
  0.0 110.3 jit_solution(3008438361731621687)
XLA Ops:
  0.6 106.1 %shard_map.128 = (bf16[2,16,4,8,384]{4,3,2,1,0:T(8,128)(2,1)}, bf16[2,16,4,8,256]{4,3,2,1,0:T(8,128)(2,1)}, bf16[320,512]{1,0:T(8,128)(2,1)}) custom-call(bf16[227,768]{1,0:T(8,128)(2,1)} %grad_in.1, bf16[768,512]{1,0:T(8,128)(2,1)} %latent_in.1, bf16[320,512]{1,0:T(8,128)(2,1)} %mesh_in.1, s32[768]{0:T(1024)} %slot_in.1, s32[3,2304]{1,0:T(4,128)} %edge_in.1, ...), custom_call_target="tpu_custom_call" | custom-call | tf_op jit(solution)/shard_map/pallas_call | solution.py:558
  106.7 3.6 %shard_map.129 = (bf16[320,512]{1,0:T(8,128)(2,1)}, f32[512,512]{1,0:T(8,128)}, f32[512,512]{1,0:T(8,128)}, f32[512,512]{1,0:T(8,128)}, f32[227,512]{1,0:T(8,128)}) custom-call(bf16[2,16,4,8,384]{4,3,2,1,0:T(8,128)(2,1)} %get-tuple-element.13.refs_0_, bf16[2,16,4,8,256]{4,3,2,1,0:T(8,128)(2,1)} %get-tuple-element.14.refs_1_, ...), custom_call_target="tpu_custom_call" | custom-call | tf_op jit(solution)/shard_map/pallas_call | solution.py:621

commit v4 on v3

--- a/solution.py
+++ b/solution.py
@@ -16,7 +16,6 @@
 NN = (((1,), (0,)), ((), ()))
 NT = (((1,), (1,)), ((), ()))
 TN = (((0,), (0,)), ((), ()))
-MIX, UNMIX = 13, 5
 
 
 def dot(a, b, dims):
@@ -28,33 +27,12 @@
     return lax.div(band, 8), lax.rem(lax.div(band, 2), 4), lax.rem(band, 2), sub
 
 
-def shifted(u, dy):
-    z, x, c, y = place()
-    z = lax.rem(z + lax.rem(u, 4), 4)
-    x = lax.rem(x + lax.rem(lax.div(u, 4), 4), 4)
-    c = lax.rem(c + lax.div(u, 16), 2)
-    return z * 8 + x * 2 + c, lax.rem(y + dy, 4)
-
-
-def near(d):
-    return shifted(lax.rem(d * MIX, 32), 0)
-
-
-def beside(d):
-    t = d - 32
-    return shifted(lax.rem(lax.div(t, 2) * MIX, 32), 1 + 2 * lax.rem(t, 2))
-
-
-def opposite(d):
-    return shifted(lax.rem((d - 96) * MIX, 32), 2)
-
-
 def source(d):
     z, x, c, y = place()
     q = jnp.where(d < 32, d, jnp.where(d < 96, (d - 32) >> 1, d - 96))
-    u = (q * MIX) & 31
     dy = jnp.where(d < 32, 0, jnp.where(d < 96, 1 + 2 * (d & 1), 2))
-    band = ((z - u) & 3) * 8 + ((x - (u >> 2)) & 3) * 2 + ((c - (u >> 4)) & 1)
+    i, o = q & 7, q >> 3
+    band = ((z - o - i) & 3) * 8 + ((x - i) & 3) * 2 + ((c - (i >> 2)) & 1)
     return band * 4 + ((y - dy) & 3)
 
 
@@ -62,14 +40,6 @@
 GROUPS = NDEV * CAP // ROWS
 BLOCKS = ROWS // MAIN
 SLOTS = NDEV * CAP
-
-
-def plane_peer(q):
-    z, x, c, y = place()
-    p = lax.rem(q * 5, 16)
-    z = lax.rem(z + lax.div(p, 4), 4)
-    x = lax.rem(x + lax.rem(p, 4), 4)
-    return (z * 8 + x * 2 + c, y), z * 4 + x
 
 
 def remote(src, dst, send, recv, device):
@@ -113,6 +83,7 @@
     main_recv,
     over_recv,
     patch,
+    patch_t,
     table,
     back,
     node,
@@ -123,14 +94,12 @@
     outer_pair,
     outer_rs_send,
     outer_rs_recv,
-    outer_ring_send,
-    outer_ring_recv,
+    outer_ring,
     inner_part,
     inner_pair,
     inner_rs_send,
     inner_rs_recv,
-    inner_ring_send,
-    inner_ring_recv,
+    inner_ring,
     psem,
     qsem,
     main_ssem,
@@ -141,6 +110,7 @@
     z, x, c, y = place()
     band = lax.axis_index("band")
     sibling = (band + 1 - 2 * c, y)
+    above, below = lax.rem(y + 1, 4), lax.rem(y + 3, 4)
     loads = [
         pltpu.make_async_copy(src, dst, load_sem.at[k])
         for k, (src, dst) in enumerate(
@@ -161,22 +131,55 @@
         load.start()
     bar = pltpu.get_barrier_semaphore()
 
-    def each(peer, act):
-        def run(d, carry):
-            act(d, peer(d))
+    def greet(n, carry):
+        to = band + n
+        to = jnp.where(to < 32, to, to - 32)
+        for k in range(4):
+            pl.semaphore_signal(bar, inc=1, device_id=(to, k), device_id_type=MESH)
+        return carry
+
+    for k in (1, 2, 3):
+        pl.semaphore_signal(
+            bar, inc=1, device_id=(band, lax.rem(y + k, 4)), device_id_type=MESH
+        )
+    lax.fori_loop(1, 32, greet, 0)
+
+    columns = [lax.rem(x + k, 4) * 2 for k in range(4)]
+    cores = [c, 1 - c]
+    cross = lax.rem(y + 2, 4)
+
+    def bands(o, first=0):
+        for i in range(first, 8):
+            yield o * 8 + i, lax.rem(z + o + i, 4) * 8 + columns[i % 4] + cores[i // 4]
+
+    def near(act):
+        for v, to in bands(0, 1):
+            act(v, (to, y))
+
+        def run(o, carry):
+            for v, to in bands(o):
+                act(v, (to, y))
             return carry
 
-        return run
-
-    def greet(d, device):
-        pl.semaphore_signal(bar, inc=1, device_id=device, device_id_type=MESH)
-
-    lax.fori_loop(1, 32, each(near, greet), 0)
-    lax.fori_loop(32, 96, each(beside, greet), 0)
-    lax.fori_loop(96, NDEV, each(opposite, greet), 0)
+        lax.fori_loop(1, 4, run, 0)
+
+    def far(act):
+        def beside(o, carry):
+            for v, to in bands(o):
+                act(32 + 2 * v, (to, above))
+                act(33 + 2 * v, (to, below))
+            return carry
+
+        def opposite(o, carry):
+            for v, to in bands(o):
+                act(96 + v, (to, cross))
+            return carry
+
+        lax.fori_loop(0, 4, beside, 0)
+        lax.fori_loop(0, 4, opposite, 0)
+
     loads[3].wait()
     pl.semaphore_wait(bar, NDEV - 1)
-    above, below = lax.rem(y + 1, 4), lax.rem(y + 3, 4)
     half = pl.ds(0, 160)
     rest = pl.ds(160, 160)
 
@@ -203,8 +206,8 @@
     j = (slot * 3641) >> 16
     r = slot - j * CAP
     dy = (j - y) & 3
-    u = (((j >> 5) - z) & 3) + 4 * (((j >> 3) - x) & 3) + 16 * (((j >> 2) - c) & 1)
-    q = (u * UNMIX) & 31
+    i = (((j >> 3) - x) & 3) + 4 * (((j >> 2) - c) & 1)
+    q = 8 * ((((j >> 5) - z) - i) & 3) + i
     d = jnp.where(dy == 0, q, jnp.where(dy == 2, 96 + q, 32 + 2 * q + (dy >> 1)))
     at_main = jnp.where(r < MAIN, d * MAIN + r, -1)
     at_over = jnp.where(r >= MAIN, d * OVER + r - MAIN, -1)
@@ -244,8 +247,8 @@
     pick_main(0)
     pick_main(1)
     main_recv[0] = main_send[0]
-    lax.fori_loop(1, 32, each(near, send_main), 0)
-    lax.fori_loop(1, 32, each(near, send_over), 0)
+    near(send_main)
+    near(send_over)
 
     def prep_group(g, carry):
         pick_main(g)
@@ -256,6 +259,10 @@
     up_half.start()
     down.wait_recv()
     down_half.start()
+    up_half.wait_recv()
+    down_half.wait_recv()
+    far(send_over)
+    far(send_main)
     back[...] = jnp.zeros_like(back)
     back[:, 0:channels] = dot(w_msg_ref[...], w_out_ref[...], NT).astype(BF)
     node[...] = jnp.zeros_like(node)
@@ -283,12 +290,6 @@
     find(0, source(line >> 1) * CAP + MAIN + (line & 1))
     lax.fori_loop(1, GROUPS, find_main, 0)
 
-    up_half.wait_recv()
-    down_half.wait_recv()
-    lax.fori_loop(32, 96, each(beside, send_over), 0)
-    lax.fori_loop(96, NDEV, each(opposite, send_over), 0)
-    lax.fori_loop(32, 96, each(beside, send_main), 0)
-    lax.fori_loop(96, NDEV, each(opposite, send_main), 0)
     for k in range(4):
         table[pl.ds(k * 320, 320), :] = dot(patch[k], w_mesh_ref[...], NN).astype(BF)
 
@@ -301,6 +302,7 @@
         return carry
 
     lax.fori_loop(0, GROUPS, collect, 0)
+    patch_t[...] = patch[...].reshape(size, 512).T
 
     def group(g):
         latent, grad = rows_ref[:, 0:512], rows_ref[:, 512:768]
@@ -380,9 +382,16 @@
     lax.fori_loop(0, GROUPS, step, 0)
 
     plane = z * 4 + x
+    planes = []
+    for k in range(1, 16):
+        n = (5 * k) % 16
+        to_z = lax.rem(z + n // 4, 4)
+        planes.append(
+            (k, (to_z * 8 + columns[n % 4] + c, y), to_z * 4 + lax.rem(x + n % 4, 4))
+        )
     scale = 1.0 / math.sqrt(3.0 * points * NDEV)
 
-    def chain(base, part, pair_recv, rs_send, rs_recv, ring_send, ring_recv, sums):
+    def chain(base, part, pair_recv, rs_send, rs_recv, ring, sums):
         width = part.shape[2]
 
         def lane(n):
@@ -391,10 +400,8 @@
         pair = remote(part.at[1 - c], pair_recv, *lane(0), sibling)
         others = pl.ds(1, 15)
         scattered = remote(rs_send.at[others], rs_recv.at[others], *lane(1), sibling)
-        three = ring_send.at[pl.ds(0, 3)]
-        ringed = remote(three, ring_recv, *lane(2), sibling)
-        lifted = sums.at[c, plane, pl.ds(0, 3)]
-        lifted = remote(lifted, lifted, *lane(3), sibling)
+        three = ring.at[pl.ds(0, 3)]
+        ringed = remote(three, three, *lane(2), sibling)
         most = sums.at[c, pl.ds(0, 15)]
         spread_out = remote(most, most, *lane(4), sibling)
         share = remote(sums.at[c], sums.at[c], *lane(5), sibling)
@@ -403,61 +410,47 @@
             pair.wait_recv()
             rs_send[...] = (part[c] + pair_recv[...]).astype(BF).reshape(16, 32, width)
 
-            def send(q, carry):
-                device, to = plane_peer(q)
-                remote(rs_send.at[to], rs_recv.at[q], *lane(1), device).start()
-                return carry
-
-            lax.fori_loop(1, 16, send, 0)
+            for k, device, to in planes:
+                remote(rs_send.at[to], rs_recv.at[k], *lane(1), device).start()
             rs_recv[0] = rs_send[plane]
 
-        def ring():
+        def circulate():
             scattered.wait_recv()
             whole = rs_recv[0].astype(F32)
             for k in range(1, 16):
                 whole += rs_recv[k].astype(F32)
-            ring_send[...] = whole.astype(BF).reshape(4, 8, width)
+            ring[y] = whole.astype(BF)
             for k in (1, 2, 3):
-                to = lax.rem(y + k, 4)
-                remote(ring_send.at[to], ring_recv.at[k - 1], *lane(2), (band, to)).start()
-
-        def lift():
+                remote(
+                    ring.at[y], ring.at[y], *lane(2), (band, lax.rem(y + k, 4))
+                ).start()
+
+        def gather():
             ringed.wait_recv()
-            whole = ring_send[y].astype(F32)
-            for k in range(3):
-                whole += ring_recv[k].astype(F32)
-            sums[c, plane, y] = (whole * scale).astype(BF)
-            block = sums.at[c, plane, y]
-            for k in (1, 2, 3):
-                remote(block, block, *lane(3), (band, lax.rem(y + k, 4))).start()
-
-        def gather():
-            lifted.wait_recv()
+            whole = ring[0].astype(F32)
+            for k in range(1, 4):
+                whole += ring[k].astype(F32)
+            sums[c, plane] = (whole * scale).astype(BF)
             block = sums.at[c, plane]
-
-            def send(q, carry):
-                device, _ = plane_peer(q)
+            for _, device, _ in planes:
                 remote(block, block, *lane(4), device).start()
-                return carry
-
-            lax.fori_loop(1, 16, send, 0)
 
         def swap():
             spread_out.wait_recv()
             share.start()
 
         def drain():
-            for copy in (pair, scattered, ringed, lifted, spread_out):
+            for copy in (pair, scattered, ringed, spread_out):
                 copy.wait_send()
             share.wait()
 
-        return pair, scatter, ring, lift, gather, swap, drain
-
-    a_pair, a_scatter, a_ring, a_lift, a_gather, a_swap, a_drain = chain(
-        4, outer_part, outer_pair, outer_rs_send, outer_rs_recv, outer_ring_send, outer_ring_recv, outer_ref
+        return pair, scatter, circulate, gather, swap, drain
+
+    a_pair, a_scatter, a_circulate, a_gather, a_swap, a_drain = chain(
+        4, outer_part, outer_pair, outer_rs_send, outer_rs_recv, outer_ring, outer_ref
     )
-    b_pair, b_scatter, b_ring, b_lift, b_gather, b_swap, b_drain = chain(
-        10, inner_part, inner_pair, inner_rs_send, inner_rs_recv, inner_ring_send, inner_ring_recv, inner_ref
+    b_pair, b_scatter, b_circulate, b_gather, b_swap, b_drain = chain(
+        10, inner_part, inner_pair, inner_rs_send, inner_rs_recv, inner_ring, inner_ref
     )
 
     def node_send_half(n, rows):
@@ -474,24 +467,19 @@
 
     a_pair.start()
     spread(GROUPS - 1)
-    for k in range(4):
-        node_send[k] = node[pl.ds(k * 320, 320), :].astype(BF)
-    a_scatter()
-    node_send_half(2, half)
-    across = dot(patch[0], node_send[0], TN)
-    for k in (1, 2, 3):
-        across += dot(patch[k], node_send[k], TN)
+    node_send[...] = node[...].astype(BF).reshape(4, 320, 512)
+    across = dot(patch_t[...], node_send[...].reshape(size, 512), NN)
     for h in range(2):
         inner_part[h] = across[:, h * 256 : h * 256 + 256]
     b_pair.start()
+    a_scatter()
+    node_send_half(2, half)
     b_scatter()
-    a_ring()
-    b_ring()
-    a_lift()
-    b_lift()
-    node_send_half(3, rest)
+    a_circulate()
+    b_circulate()
     a_gather()
     b_gather()
+    node_send_half(3, rest)
     first, second = node_wait(2, half), node_wait(3, rest)
     first.wait_recv()
     second.wait_recv()
@@ -559,8 +547,8 @@
         kernel,
         in_specs=[hbm] * 9,
         out_shape=[
-            jax.ShapeDtypeStruct((2, 16, 4, 8, 384), BF),
-            jax.ShapeDtypeStruct((2, 16, 4, 8, 256), BF),
+            jax.ShapeDtypeStruct((2, 16, 32, 384), BF),
+            jax.ShapeDtypeStruct((2, 16, 32, 256), BF),
             jax.ShapeDtypeStruct((320, 512), BF),
         ],
         scratch_shapes=[
@@ -581,6 +569,7 @@
             vmem((NDEV, MAIN, 768), BF),
             vmem((NDEV, OVER, 768), BF),
             vmem((4, 320, 512), BF),
+            vmem((512, 1280), BF),
             vmem((1280, 512), BF),
             vmem((512, 256), BF),
             vmem((1280, 512), F32),
@@ -591,14 +580,12 @@
             vmem((512, 384), F32),
             vmem((16, 32, 384), BF),
             vmem((16, 32, 384), BF),
-            vmem((4, 8, 384), BF),
-            vmem((3, 8, 384), BF),
+            vmem((4, 32, 384), BF),
             vmem((2, 512, 256), F32),
             vmem((512, 256), F32),
             vmem((16, 32, 256), BF),
             vmem((16, 32, 256), BF),
-            vmem((4, 8, 256), BF),
-            vmem((3, 8, 256), BF),
+            vmem((4, 32, 256), BF),
             pltpu.SemaphoreType.DMA((4,)),
             pltpu.SemaphoreType.DMA((4,)),
             pltpu.SemaphoreType.DMA((1,)),

time: 110 us -> 103 us (0.936)
  Pallas kernels: 110 us -> 102 us
    pallas_call x1, Pallas kernels: 106 us -> 98.6 us  [shards(): pl.pallas_call(kernel, in_specs=[hbm] * 9, out_shape=[jax.ShapeDtypeStruc...]
where the time goes in v4:
time: 103 us
  Pallas kernels  102 us (99%)
    pallas_call x1, Pallas kernels, shards(): pl.pallas_call(kernel, in_specs=[hbm] * 9, out_shape=[jax.ShapeDtypeStruc...  98.6 us
    pallas_call x1, Pallas kernels, shards(): pl.pallas_call(final_kernel, out_shape=[jax.ShapeDtypeStruct(*shape) for...  3.55 us

profile of v4, /device:TPU:1, one launch (start us, length us, event | category | flops | bytes accessed | tf_op | source)
XLA Modules:
  0.0 102.8 jit_solution(7020424149842678094)
XLA Ops:
  0.6 98.6 %shard_map.128 = (bf16[2,16,32,384]{3,2,1,0:T(8,128)(2,1)}, bf16[2,16,32,256]{3,2,1,0:T(8,128)(2,1)}, bf16[320,512]{1,0:T(8,128)(2,1)}) custom-call(bf16[227,768]{1,0:T(8,128)(2,1)} %grad_in.1, bf16[768,512]{1,0:T(8,128)(2,1)} %latent_in.1, bf16[320,512]{1,0:T(8,128)(2,1)} %mesh_in.1, s32[768]{0:T(1024)} %slot_in.1, s32[3,2304]{1,0:T(4,128)} %edge_in.1, ...), custom_call_target="tpu_custom_call" | custom-call | tf_op jit(solution)/shard_map/pallas_call | solution.py:546
  99.2 3.6 %shard_map.129 = (bf16[320,512]{1,0:T(8,128)(2,1)}, f32[512,512]{1,0:T(8,128)}, f32[512,512]{1,0:T(8,128)}, f32[512,512]{1,0:T(8,128)}, f32[227,512]{1,0:T(8,128)}) custom-call(bf16[2,16,32,384]{3,2,1,0:T(8,128)(2,1)} %get-tuple-element.13.refs_0_, bf16[2,16,32,256]{3,2,1,0:T(8,128)(2,1)} %get-tuple-element.14.refs_1_, ...), custom_call_target="tpu_custom_call" | custom-call | tf_op jit(solution)/shard_map/pallas_call | solution.py:608

commit v5 on v4

--- a/solution.py
+++ b/solution.py
@@ -186,13 +186,15 @@
     def patch_copy(n, block, to):
         return remote(block, block, psem.at[n], qsem.at[n], (band, to))
 
-    up = patch_copy(0, patch.at[y], above)
-    down = patch_copy(1, patch.at[y], below)
+    up = patch_copy(0, patch.at[y, rest], above)
+    down = patch_copy(1, patch.at[y, half], below)
+    up_later = patch_copy(4, patch.at[y, half], above)
+    down_later = patch_copy(5, patch.at[y, rest], below)
     up_half = patch_copy(2, patch.at[below, rest], above)
     down_half = patch_copy(3, patch.at[above, half], below)
-    up.start()
-    down.start()
-    for k in (0, 1, 2, 4, 5, 6, 7, 8):
+    for copy in (up, down, up_later, down_later):
+        copy.start()
+    for k in (0, 1, 2):
         loads[k].wait()
     channels, points = grad_ref.shape
     me = band * 4 + y
@@ -259,10 +261,10 @@
     up_half.start()
     down.wait_recv()
     down_half.start()
-    up_half.wait_recv()
-    down_half.wait_recv()
     far(send_over)
     far(send_main)
+    for k in (4, 5, 6, 7, 8):
+        loads[k].wait()
     back[...] = jnp.zeros_like(back)
     back[:, 0:channels] = dot(w_msg_ref[...], w_out_ref[...], NT).astype(BF)
     node[...] = jnp.zeros_like(node)
@@ -290,6 +292,10 @@
     find(0, source(line >> 1) * CAP + MAIN + (line & 1))
     lax.fori_loop(1, GROUPS, find_main, 0)
 
+    up_half.wait_recv()
+    down_half.wait_recv()
+    up_later.wait_recv()
+    down_later.wait_recv()
     for k in range(4):
         table[pl.ds(k * 320, 320), :] = dot(patch[k], w_mesh_ref[...], NN).astype(BF)
 
@@ -480,6 +486,8 @@
     a_gather()
     b_gather()
     node_send_half(3, rest)
+    a_swap()
+    b_swap()
     first, second = node_wait(2, half), node_wait(3, rest)
     first.wait_recv()
     second.wait_recv()
@@ -487,10 +495,8 @@
     proj_ref[...] = (
         mine + node_recv[0].astype(F32) + node_recv[1].astype(F32) + node_recv[2].astype(F32)
     ).astype(BF)
-    a_swap()
-    b_swap()
-
-    for copy in (up, down, up_half, down_half, first, second):
+
+    for copy in (up, down, up_later, down_later, up_half, down_half, first, second):
         copy.wait_send()
     blocks = pl.ds(1, NDEV - 1)
     remote(over_send.at[blocks], over_recv.at[blocks], ssem.at[1], rsem.at[1], sibling).wait_send()
@@ -586,8 +592,8 @@
             vmem((16, 32, 256), BF),
             vmem((16, 32, 256), BF),
             vmem((4, 32, 256), BF),
-            pltpu.SemaphoreType.DMA((4,)),
-            pltpu.SemaphoreType.DMA((4,)),
+            pltpu.SemaphoreType.DMA((6,)),
+            pltpu.SemaphoreType.DMA((6,)),
             pltpu.SemaphoreType.DMA((1,)),
             pltpu.SemaphoreType.DMA((GROUPS - 1,)),
             pltpu.SemaphoreType.DMA((16,)),

time: 103 us -> 99 us (0.961)
  Pallas kernels: 102 us -> 98.2 us
    pallas_call x1, Pallas kernels: 98.6 us -> 94.7 us  [shards(): pl.pallas_call(kernel, in_specs=[hbm] * 9, out_shape=[jax.ShapeDtypeStruc...]
where the time goes in v5:
time: 99 us; the launch traced here: 98.8 us
  Pallas kernels  98.2 us (99%)
    pallas_call x1, Pallas kernels, shards(): pl.pallas_call(kernel, in_specs=[hbm] * 9, out_shape=[jax.ShapeDtypeStruc...  94.7 us
    pallas_call x1, Pallas kernels, shards(): pl.pallas_call(final_kernel, out_shape=[jax.ShapeDtypeStruct(*shape) for...  3.55 us

profile of v5, /device:TPU:1, one launch (start us, length us, event | category | flops | bytes accessed | tf_op | source)
XLA Modules:
  0.0 98.8 jit_solution(14311774485230845439)
XLA Ops:
  0.6 94.7 %shard_map.128 = (bf16[2,16,32,384]{3,2,1,0:T(8,128)(2,1)}, bf16[2,16,32,256]{3,2,1,0:T(8,128)(2,1)}, bf16[320,512]{1,0:T(8,128)(2,1)}) custom-call(bf16[227,768]{1,0:T(8,128)(2,1)} %grad_in.1, bf16[768,512]{1,0:T(8,128)(2,1)} %latent_in.1, bf16[320,512]{1,0:T(8,128)(2,1)} %mesh_in.1, s32[768]{0:T(1024)} %slot_in.1, s32[3,2304]{1,0:T(4,128)} %edge_in.1, ...), custom_call_target="tpu_custom_call" | custom-call | tf_op jit(solution)/shard_map/pallas_call | solution.py:552
  95.3 3.5 %shard_map.129 = (bf16[320,512]{1,0:T(8,128)(2,1)}, f32[512,512]{1,0:T(8,128)}, f32[512,512]{1,0:T(8,128)}, f32[512,512]{1,0:T(8,128)}, f32[227,512]{1,0:T(8,128)}) custom-call(bf16[2,16,32,384]{3,2,1,0:T(8,128)(2,1)} %get-tuple-element.13.refs_0_, bf16[2,16,32,256]{3,2,1,0:T(8,128)(2,1)} %get-tuple-element.14.refs_1_, ...), custom_call_target="tpu_custom_call" | custom-call | tf_op jit(solution)/shard_map/pallas_call | solution.py:614
